TPU v7x, 256 devices: a whole 4x4x8 slice. The times are simulated.
256 devices in a mesh: shot: 4 (over x_lo, core), tile: 64 (over x_hi, z, y).
Axes of the slice: x: 4 (x_hi: 2, x_lo: 2; x = x_hi * 2 + x_lo), y: 4, z: 8, core: 2. Of those that a mesh axis runs over, the one named last changes fastest.
Arguments:
- partials: bfloat16 [256, 8, 512, 512], P(('shot', 'tile')), may hold values from -6 to 6
Outputs:
- filtered: float32 [8, 512, 512], P('shot', 'tile')
All inputs are finite; a program needn't handle non-finite values.
Results may differ from a plain program's by a relative error of at most 0.0003.
Values may be sent and summed in bfloat16 or wider, within the bound.
A program may use at most 64 MiB of HBM per device.

v0:
```python
import jax
import jax.numpy as jnp
from jax import lax
from jax.sharding import PartitionSpec as P


def copy_for_each(value, axis):
    copies = jnp.broadcast_to(value, (lax.axis_size(axis), *value.shape))
    return lax.all_to_all(copies, axis, split_axis=0, concat_axis=0, tiled=True)


def over_copies(value, axis):
    return copy_for_each(value, axis).sum(axis=0)


def extended(value, sides, width):
    edges = {}
    for axis, dim in sides:
        devices, length = (lax.axis_size(axis), value.shape[dim])
        up = [(i, (i + 1) % devices) for i in range(devices - 1)]
        last = lax.slice_in_dim(value, length - width, length, axis=dim)
        first = lax.slice_in_dim(value, 0, width, axis=dim)
        edges[dim] = (
            lax.ppermute(last, axis, up),
            lax.ppermute(first, axis, [(b, a) for a, b in up]),
        )
    done = []
    for _, dim in sides:
        low, high = edges[dim]
        around = [(width, width) if d in done else (0, 0) for d in range(value.ndim)]
        value = jnp.concatenate([jnp.pad(low, around), value, jnp.pad(high, around)], axis=dim)
        done.append(dim)
    return value


def body(partials):
    groups = lax.axis_size("shot")
    members = lax.axis_size("tile")
    depth_all = partials.shape[1]
    depth_part = depth_all // groups
    moved = lax.all_to_all(partials, "tile", split_axis=2, concat_axis=0, tiled=True)
    strip = jnp.sum(moved, axis=0, dtype=jnp.float32)
    full = over_copies(strip, "shot")
    offset = lax.axis_index("shot") * depth_part
    block = lax.dynamic_slice_in_dim(full, offset, depth_part, 0)
    image = block / jnp.sqrt(jnp.float32(groups * members))
    padded = extended(image, (("shot", 0), ("tile", 1)), 1)
    padded = jnp.pad(padded, ((0, 0), (0, 0), (1, 1)))
    beside = padded[2:, 1:-1, 1:-1] + padded[:-2, 1:-1, 1:-1]
    beside = beside + padded[1:-1, 2:, 1:-1] + padded[1:-1, :-2, 1:-1]
    beside = beside + padded[1:-1, 1:-1, 2:] + padded[1:-1, 1:-1, :-2]
    return 6.0 * image - beside


def solution(mesh):
    return jax.shard_map(
        body,
        mesh=mesh,
        in_specs=(P(("shot", "tile"), None, None, None),),
        out_specs=P("shot", "tile", None),
        check_vma=False,
    )
```

profile of v0, /device:TPU:6, one launch (start us, length us, event | category | flops | bytes accessed | tf_op | source)
XLA Modules:
  0.0 151.8 jit_solution(5048527065460529649)
XLA Ops:
  0.0 4.5 %copy.5 = bf16[1,8,512,512]{3,1,0,2:T(8,128)(2,1)S(1)} copy(bf16[1,8,512,512]{3,2,1,0:T(8,128)(2,1)} %param.1) | data formatting | bytes 8388608 | tf_op args[0]
  4.5 108.4 %all_to_all.14 = bf16[1,8,512,512]{3,1,0,2:T(8,128)(2,1)S(1)} all-to-all(bf16[1,8,512,512]{3,1,0,2:T(8,128)(2,1)S(1)} %copy.5), channel_id=1, replica_groups=mesh['shot'=4,'tile'=64] {'tile'}, dimensions={2} | all-to-all | bytes 8388608 | tf_op jit(solution)/shard_map/all_to_all | solution.py:41
  112.9 0.6 convert_reduce_fusion
  113.6 0.1 copy.6
  113.6 0.9 broadcast_in_dim.3
  114.5 4.3 %all-to-all-start.1 = ((f32[4,8,8,512]{3,2,1,0:T(8,128)}), f32[4,8,8,512]{3,2,1,0:T(8,128)S(1)}, u32[]{:S(2)}, u32[]{:S(2)}) async-start(f32[4,8,8,512]{3,2,1,0:T(8,128)} %broadcast_in_dim.3), calls=%async_computation.1 | async-start | bytes 1048576 | tf_op jit(solution)/shard_map/all_to_all | solution.py:9
  118.8 7.2 %all-to-all-done.1 = f32[4,8,8,512]{3,2,1,0:T(8,128)S(1)} async-done(((f32[4,8,8,512]{3,2,1,0:T(8,128)}), f32[4,8,8,512]{3,2,1,0:T(8,128)S(1)}, u32[]{:S(2)}, u32[]{:S(2)}) %all-to-all-start.1) | async-done | bytes 524320 | tf_op jit(solution)/shard_map/all_to_all | solution.py:9
  126.0 2.7 %collective-permute-start = (f32[1,8,512]{2,1,0:T(8,128)S(1)}, f32[1,8,512]{2,1,0:T(8,128)S(1)}, u32[]{:S(2)}, u32[]{:S(2)}) collective-permute-start(f32[1,8,512]{2,1,0:T(8,128)S(1)} %get-tuple-element.6), channel_id=1, source_target_pairs={{64,0},{128,64},{192,128},{65,1},{129,65},{193,129},{66,2},{130,66... | collective-permute-start | bytes 49160 | tf_op jit(solution)/shard_map/ppermute | solution.py:25
  128.7 1.9 %collective-permute-start.1 = (f32[1,8,512]{2,1,0:T(8,128)S(1)}, f32[1,8,512]{2,1,0:T(8,128)S(1)}, u32[]{:S(2)}, u32[]{:S(2)}) collective-permute-start(f32[1,8,512]{2,1,0:T(8,128)S(1)} %get-tuple-element.5), channel_id=1, source_target_pairs={{0,64},{64,128},{128,192},{1,65},{65,129},{129,193},{2,66},{66,130... | collective-permute-start | bytes 49160 | tf_op jit(solution)/shard_map/ppermute | solution.py:24
  130.7 9.0 %collective-permute-start.2 = (f32[2,1,512]{2,1,0:T(1,128)S(1)}, f32[2,1,512]{2,1,0:T(1,128)S(1)}, u32[]{:S(2)}, u32[]{:S(2)}) collective-permute-start(f32[2,1,512]{2,1,0:T(1,128)S(1)} %get-tuple-element.8), channel_id=1, source_target_pairs={{1,0},{2,1},{3,2},{4,3},{5,4},{6,5},{7,6},{8,7},{9,8},{10,9},{11,1... | collective-permute-start | bytes 12296 | tf_op jit(solution)/shard_map/ppermute | solution.py:25
  139.7 1.9 %collective-permute-start.3 = (f32[2,1,512]{2,1,0:T(1,128)S(1)}, f32[2,1,512]{2,1,0:T(1,128)S(1)}, u32[]{:S(2)}, u32[]{:S(2)}) collective-permute-start(f32[2,1,512]{2,1,0:T(1,128)S(1)} %get-tuple-element.7), channel_id=1, source_target_pairs={{0,1},{1,2},{2,3},{3,4},{4,5},{5,6},{6,7},{7,8},{8,9},{9,10},{10,1... | collective-permute-start | bytes 12296 | tf_op jit(solution)/shard_map/ppermute | solution.py:24
  141.6 0.0 collective-permute-done.2
  141.7 9.3 %collective-permute-done.3 = f32[2,1,512]{2,1,0:T(1,128)S(1)} collective-permute-done((f32[2,1,512]{2,1,0:T(1,128)S(1)}, f32[2,1,512]{2,1,0:T(1,128)S(1)}, u32[]{:S(2)}, u32[]{:S(2)}) %collective-permute-start.3) | collective-permute-done | bytes 4128 | tf_op jit(solution)/shard_map/ppermute | solution.py:24
  150.9 0.0 collective-permute-done
  151.0 0.0 collective-permute-done.1
  151.0 0.2 select_maximum_fusion
  151.1 0.7 fusion.1
  (6 shorter events, 0.1 us)
Async XLA Ops:
  114.5 11.4 %all-to-all-start.1 = ((f32[4,8,8,512]{3,2,1,0:T(8,128)}), f32[4,8,8,512]{3,2,1,0:T(8,128)S(1)}, u32[]{:S(2)}, u32[]{:S(2)}) async-start(f32[4,8,8,512]{3,2,1,0:T(8,128)} %broadcast_in_dim.3), calls=%async_computation.1 | async-start | bytes 1048576 | tf_op jit(solution)/shard_map/all_to_all | solution.py:9
  126.0 24.9 %collective-permute-start = (f32[1,8,512]{2,1,0:T(8,128)S(1)}, f32[1,8,512]{2,1,0:T(8,128)S(1)}, u32[]{:S(2)}, u32[]{:S(2)}) collective-permute-start(f32[1,8,512]{2,1,0:T(8,128)S(1)} %get-tuple-element.6), channel_id=1, source_target_pairs={{64,0},{128,64},{192,128},{65,1},{129,65},{193,129},{66,2},{130,66... | collective-permute-start | bytes 49160 | tf_op jit(solution)/shard_map/ppermute | solution.py:25
  128.7 22.2 %collective-permute-start.1 = (f32[1,8,512]{2,1,0:T(8,128)S(1)}, f32[1,8,512]{2,1,0:T(8,128)S(1)}, u32[]{:S(2)}, u32[]{:S(2)}) collective-permute-start(f32[1,8,512]{2,1,0:T(8,128)S(1)} %get-tuple-element.5), channel_id=1, source_target_pairs={{0,64},{64,128},{128,192},{1,65},{65,129},{129,193},{2,66},{66,130... | collective-permute-start | bytes 49160 | tf_op jit(solution)/shard_map/ppermute | solution.py:24
  130.7 11.0 %collective-permute-start.2 = (f32[2,1,512]{2,1,0:T(1,128)S(1)}, f32[2,1,512]{2,1,0:T(1,128)S(1)}, u32[]{:S(2)}, u32[]{:S(2)}) collective-permute-start(f32[2,1,512]{2,1,0:T(1,128)S(1)} %get-tuple-element.8), channel_id=1, source_target_pairs={{1,0},{2,1},{3,2},{4,3},{5,4},{6,5},{7,6},{8,7},{9,8},{10,9},{11,1... | collective-permute-start | bytes 12296 | tf_op jit(solution)/shard_map/ppermute | solution.py:25
  139.7 11.2 %collective-permute-start.3 = (f32[2,1,512]{2,1,0:T(1,128)S(1)}, f32[2,1,512]{2,1,0:T(1,128)S(1)}, u32[]{:S(2)}, u32[]{:S(2)}) collective-permute-start(f32[2,1,512]{2,1,0:T(1,128)S(1)} %get-tuple-element.7), channel_id=1, source_target_pairs={{0,1},{1,2},{2,3},{3,4},{4,5},{5,6},{6,7},{7,8},{8,9},{9,10},{10,1... | collective-permute-start | bytes 12296 | tf_op jit(solution)/shard_map/ppermute | solution.py:24
where the time goes:
time: 152 us
  blocking collectives  108 us (71%)
  starting transfers between devices  19.8 us (13%)
  waiting for transfers between devices  16.5 us (11%)
  local copies, waits for them, and re-layouts  5.49 us (4%)
  other arithmetic  1.54 us (1%)
    all_to_all x1, blocking collectives, body(): lax.all_to_all(partials, 'tile', split_axis=2, concat_axis=0, tiled=True)  108 us
    ppermute x2, starting transfers between devices, extended(): lax.ppermute(first, axis, [(b, a) for a, b in up])  11.7 us
    ppermute x2, waiting for transfers between devices, extended(): lax.ppermute(last, axis, up)  9.27 us
    all_to_all x1, waiting for transfers between devices, copy_for_each(): return lax.all_to_all(copies, axis, split_axis=0, concat_axis=0, tiled=True)  7.18 us
    unnamed x1, local copies, waits for them, and re-layouts  4.53 us
    all_to_all x1, starting transfers between devices, copy_for_each(): return lax.all_to_all(copies, axis, split_axis=0, concat_axis=0, tiled=True)  4.27 us
    ppermute x2, starting transfers between devices, extended(): lax.ppermute(last, axis, up)  3.84 us
  transfers between devices with their start and end apart: 5, of which 2 were waited for; matrix products, arithmetic and copies ran while one was open for 0% of the time, Pallas kernels for 0%

commit v1 on v0

v1 whole, which is shorter than its diff:
```python
import functools

import jax
import jax.numpy as jnp
from jax import lax
from jax.experimental import pallas as pl
from jax.experimental.pallas import tpu as pltpu
from jax.sharding import PartitionSpec as P

MESH = pl.DeviceIdType.MESH
NCH = 2
NY = 512
CW = NY // NCH
F32 = jnp.float32
BF16 = jnp.bfloat16


def kernel(scale, pa, pb, out, own, sib, rel, dirt, cout, cin, S, qrel, qdir, qout, qin, T, zin, img, rows, deps,
           own_sem, sib_s, sib_r, rel_s, rel_r, dir_s, dir_r, c_s, c_r, qrel_s, qrel_r, qdir_s, qdir_r, qc_s, qc_r,
           z_s, z_r, row_s, row_r, dep_s, dep_r):
    s, t = lax.axis_index("shot"), lax.axis_index("tile")
    core, xl = lax.rem(s, 2), s // 2
    xh, z, y = t // 32, lax.rem(t // 4, 8), lax.rem(t, 4)
    X = xh * 2 + xl

    def at(Xq, zq, yq, cq):
        return (lax.rem(Xq, 2) * 2 + cq, (Xq // 2) * 32 + zq * 4 + yq)

    def wrap(v, n):
        return lax.rem(v + n, n)

    def peer(g, step, cq):
        if g == 0:
            return at(wrap(X + step, 4), z, y, cq)
        return at(X, z, wrap(y + step, 4), cq)

    other = 1 - core
    ring = lambda d, n, p: lax.rem(p + d + n, n)
    neighbours = [(s + 1 - 2 * core, t)]
    for g in range(2):
        for step in (1, -1):
            for cq in range(2):
                neighbours.append(peer(g, step, cq))
    for k in range(1, 8):
        neighbours.append(at(X, ring(k, 8, z), y, core))
    neighbours.append((s, ring(1, 64, t)))
    neighbours.append((s, ring(-1, 64, t)))
    barrier = pltpu.get_barrier_semaphore()
    for dev in neighbours:
        pl.semaphore_signal(barrier, inc=1, device_id=dev, device_id_type=MESH)
    pl.semaphore_wait(barrier, len(neighbours))

    sends = []

    def send(src, dst, ss, rs, dev):
        cp = pltpu.make_async_remote_copy(src_ref=src, dst_ref=dst, send_sem=ss, recv_sem=rs, device_id=dev,
                                          device_id_type=MESH)
        cp.start()
        sends.append(cp)
        return cp

    def wait_in(dst, rs):
        pltpu.make_async_copy(dst, dst, rs).wait()

    def raw(g, ch, step, cq, h):
        cols = pl.ds(ch * CW, CW)
        if g == 0:
            Xq = wrap(X + step, 4)
            return pa.at[2 * (lax.rem(Xq, 2) * 2 + cq), pl.ds(32 * (Xq // 2) + 16 * h, 16), :, cols]
        return pb.at[2 * (h * 2 + cq) + 1, :, wrap(y + step, 4), :, cols]

    PIECES = ((1, 0), (-1, 1), (0, 0), (0, 1))

    def raw_relay(g, ch):
        for d, step in enumerate((1, -1)):
            for cq in range(2):
                send(raw(g, ch, 2, cq, d), rel.at[g, ch, d, core], rel_s.at[g, ch, d, cq], rel_r.at[g, ch, d, core],
                     peer(g, step, cq))

    def raw_direct(g, ch):
        for d, step in enumerate((1, -1)):
            for cq in range(2):
                send(raw(g, ch, step, cq, 1 - d), dirt.at[g, ch, d, core], dir_s.at[g, ch, d, cq],
                     dir_r.at[g, ch, d, core], peer(g, step, cq))

    def raw_pair(g, ch):
        for i, (step, h) in enumerate(PIECES):
            pltpu.make_async_copy(raw(g, ch, step, core, h), own.at[g, ch, i], own_sem.at[g, ch, i]).start()
            send(raw(g, ch, step, other, h), sib.at[g, ch, i], sib_s.at[g, ch, i], sib_r.at[g, ch, i],
                 (s + 1 - 2 * core, t))

    def wait_pair(g, ch, i):
        wait_in(own.at[g, ch, i], own_sem.at[g, ch, i])
        wait_in(sib.at[g, ch, i], sib_r.at[g, ch, i])

    def add(ref, *idx):
        return ref[idx].astype(F32)

    def combine(g, ch):
        for d, step in enumerate((1, -1)):
            wait_pair(g, ch, d)
            for cq in range(2):
                wait_in(rel.at[g, ch, d, cq], rel_r.at[g, ch, d, cq])

            @pl.loop(0, 16)
            def _(i):
                cout[g, ch, d, i] = (add(own, g, ch, d, i) + add(sib, g, ch, d, i)) + (
                    add(rel, g, ch, d, 0, i) + add(rel, g, ch, d, 1, i))

            send(cout.at[g, ch, d], cin.at[g, ch, d], c_s.at[g, ch, d], c_r.at[g, ch, d], peer(g, step, core))

    def first_sum(g, ch):
        for h in range(2):
            wait_pair(g, ch, 2 + h)
            for cq in range(2):
                wait_in(dirt.at[g, ch, 1 - h, cq], dir_r.at[g, ch, 1 - h, cq])
            wait_in(cin.at[g, ch, h], c_r.at[g, ch, h])

            @pl.loop(0, 4)
            def _(i):
                for j in range(4):
                    k = i * 4 + j
                    S[g, ch, h, i, j] = ((add(own, g, ch, 2 + h, k) + add(sib, g, ch, 2 + h, k)) + (
                        add(dirt, g, ch, 1 - h, 0, k) + add(dirt, g, ch, 1 - h, 1, k))) + cin[g, ch, h, k]

    def qblock(g, ch, step, h):
        if g == 0:
            return S.at[g, ch, h, :, wrap(y + step, 4)]
        Xq = wrap(X + step, 4)
        return S.at[g, ch, lax.rem(Xq, 2), (Xq // 2) * 2 + h]

    def second_raw(g, ch):
        for d, step in enumerate((1, -1)):
            dev = peer(1 - g, step, core)
            send(qblock(g, ch, 2, d), qrel.at[g, ch, d], qrel_s.at[g, ch, d], qrel_r.at[g, ch, d], dev)
        for d, step in enumerate((1, -1)):
            dev = peer(1 - g, step, core)
            send(qblock(g, ch, step, 1 - d), qdir.at[g, ch, d], qdir_s.at[g, ch, d], qdir_r.at[g, ch, d], dev)

    def second_combine(g, ch):
        for d, step in enumerate((1, -1)):
            wait_in(qrel.at[g, ch, d], qrel_r.at[g, ch, d])
            qout[g, ch, d] = qrel[g, ch, d] + qblock(g, ch, step, d)[...]
            send(qout.at[g, ch, d], qin.at[g, ch, d], qc_s.at[g, ch, d], qc_r.at[g, ch, d], peer(1 - g, step, core))

    def second_sum(g, ch):
        for h in range(2):
            wait_in(qdir.at[g, ch, 1 - h], qdir_r.at[g, ch, 1 - h])
            wait_in(qin.at[g, ch, h], qc_r.at[g, ch, h])
            total = (qdir[g, ch, 1 - h] + qin[g, ch, h]) + qblock(g, ch, 0, h)[...]
            for j in range(4):
                T[ch, 4 * h + j, g] = total[j]

    def third_send(ch):
        for k in range(1, 8):
            zq = ring(k, 8, z)
            send(T.at[ch, zq], zin.at[ch, k - 1], z_s.at[ch, k - 1], z_r.at[ch, k - 1], at(X, zq, y, core))

    def third_sum(ch):
        total = T[ch, z]
        for k in range(1, 8):
            wait_in(zin.at[ch, k - 1], z_r.at[ch, k - 1])
            total = total + zin[ch, k - 1]
        img[:, :, ch * CW:(ch + 1) * CW] = total * scale

    both = ((0,), (1,))
    for g in range(2):
        raw_relay(g, 0)
    for g in range(2):
        raw_pair(g, 0)
    for g in range(2):
        raw_direct(g, 0)
    for ch in range(1, NCH):
        for g in range(2):
            raw_relay(g, ch)
        for g in range(2):
            raw_pair(g, ch)
    for ch in range(NCH):
        for g in range(2):
            combine(g, ch)
        if ch + 1 < NCH:
            for g in range(2):
                raw_direct(g, ch + 1)
        for g in range(2):
            first_sum(g, ch)
            second_raw(g, ch)
        for g in range(2):
            second_combine(g, ch)
        for g in range(2):
            second_sum(g, ch)
        third_send(ch)
    for ch in range(NCH):
        third_sum(ch)

    for d, step in enumerate((1, -1)):
        send(img, rows.at[d], row_s.at[d], row_r.at[d], (s, ring(step, 64, t)))
        send(img.at[1 - d], deps.at[d], dep_s.at[d], dep_r.at[d], (ring(step, 4, s), t))

    for d in range(2):
        wait_in(rows.at[d], row_r.at[d])
        wait_in(deps.at[d], dep_r.at[d])
    below = jnp.where(s > 0, 1.0, 0.0).astype(F32)
    above = jnp.where(s < 3, 1.0, 0.0).astype(F32)
    left = jnp.where(t > 0, 1.0, 0.0).astype(F32)
    right = jnp.where(t < 63, 1.0, 0.0).astype(F32)
    lane = lax.broadcasted_iota(jnp.int32, (8, NY), 1)
    for p in range(2):
        v = img[p]
        if p == 0:
            beside = deps[0] * below + img[1]
        else:
            beside = deps[1] * above + img[0]
        prev = jnp.concatenate([rows[0, p, 7:8] * left, v[:7]], axis=0)
        following = jnp.concatenate([v[1:], rows[1, p, 0:1] * right], axis=0)
        beside = beside + prev + following
        beside = beside + jnp.where(lane == 0, 0.0, pltpu.roll(v, 1, 1))
        beside = beside + jnp.where(lane == NY - 1, 0.0, pltpu.roll(v, NY - 1, 1))
        out[p] = 6.0 * v - beside
    for cp in sends:
        cp.wait_send()


def solution(mesh):
    shots = mesh.shape["shot"] * mesh.shape["tile"]
    scale = 1.0 / float(shots) ** 0.5
    D = pltpu.SemaphoreType.DMA
    V = pltpu.VMEM

    def step(partials):
        pa = partials.reshape(8, 64, 8, NY)
        pb = partials.reshape(8, 16, 4, 8, NY)
        return pl.pallas_call(
            functools.partial(kernel, scale),
            out_shape=jax.ShapeDtypeStruct((2, 8, NY), F32),
            in_specs=[pl.BlockSpec(memory_space=pl.ANY)] * 2,
            out_specs=pl.BlockSpec(memory_space=pltpu.VMEM),
            scratch_shapes=[
                V((2, NCH, 4, 16, 8, CW), BF16),
                V((2, NCH, 4, 16, 8, CW), BF16),
                V((2, NCH, 2, 2, 16, 8, CW), BF16),
                V((2, NCH, 2, 2, 16, 8, CW), BF16),
                V((2, NCH, 2, 16, 8, CW), F32),
                V((2, NCH, 2, 16, 8, CW), F32),
                V((2, NCH, 2, 4, 4, 8, CW), F32),
                V((2, NCH, 2, 4, 8, CW), F32),
                V((2, NCH, 2, 4, 8, CW), F32),
                V((2, NCH, 2, 4, 8, CW), F32),
                V((2, NCH, 2, 4, 8, CW), F32),
                V((NCH, 8, 2, 8, CW), F32),
                V((NCH, 7, 2, 8, CW), F32),
                V((2, 8, NY), F32),
                V((2, 2, 8, NY), F32),
                V((2, 8, NY), F32),
                D((2, NCH, 4)),
                D((2, NCH, 4)), D((2, NCH, 4)),
                D((2, NCH, 2, 2)), D((2, NCH, 2, 2)),
                D((2, NCH, 2, 2)), D((2, NCH, 2, 2)),
                D((2, NCH, 2)), D((2, NCH, 2)),
                D((2, NCH, 2)), D((2, NCH, 2)),
                D((2, NCH, 2)), D((2, NCH, 2)),
                D((2, NCH, 2)), D((2, NCH, 2)),
                D((NCH, 7)), D((NCH, 7)),
                D((2,)), D((2,)),
                D((2,)), D((2,)),
            ],
            compiler_params=pltpu.CompilerParams(collective_id=0, has_side_effects=True,
                                                 vmem_limit_bytes=48 * 1024 * 1024),
        )(pa, pb)

    return jax.shard_map(step, mesh=mesh, in_specs=(P(("shot", "tile"), None, None, None),),
                         out_specs=P("shot", "tile", None), check_vma=False)
```

time: 152 us -> 59.6 us (0.39)
  the two profiles are of different devices: /device:TPU:6 before, /device:TPU:2 now
where the time goes in v1:
time: 59.6 us; the launch traced here: 59.5 us
  Pallas kernels  56.6 us (95%)
  local copies, waits for them, and re-layouts  2.8 us (5%)
    pallas_call x1, Pallas kernels, step(): pl.pallas_call(functools.partial(kernel, scale), out_shape=jax.ShapeDtype...  56.6 us
    unnamed x3, local copies, waits for them, and re-layouts  2.8 us

profile of v1, /device:TPU:2, one launch (start us, length us, event | category | flops | bytes accessed | tf_op | source)
XLA Modules:
  0.0 59.5 jit_solution(291384228741879550)
XLA Ops:
  0.0 0.0 copy-start
  0.0 2.2 %copy-done = bf16[1,8,512,512]{3,2,1,0:T(8,128)(2,1)S(1)} copy-done((bf16[1,8,512,512]{3,2,1,0:T(8,128)(2,1)S(1)}, bf16[1,8,512,512]{3,2,1,0:T(8,128)(2,1)}, u32[]{:S(2)}) %copy-start) | copy-done | bytes 4194328
  2.2 56.6 %shard_map.17 = f32[2,8,512]{2,1,0:T(8,128)S(1)} custom-call(bf16[8,64,8,512]{3,2,1,0:T(8,128)(2,1)S(1)} %bitcast.2, bf16[8,16,4,8,512]{4,3,2,1,0:T(8,128)(2,1)S(1)} %bitcast.3), custom_call_target="tpu_custom_call" | custom-call | tf_op jit(solution)/shard_map/pallas_call | solution.py:232
  58.8 0.6 %copy.3 = f32[2,8,512]{2,1,0:T(8,128)} copy(f32[2,8,512]{2,1,0:T(8,128)S(1)} %shard_map.17) | data formatting | bytes 65536
Async XLA Ops:
  0.0 2.2 %copy-start = (bf16[1,8,512,512]{3,2,1,0:T(8,128)(2,1)S(1)}, bf16[1,8,512,512]{3,2,1,0:T(8,128)(2,1)}, u32[]{:S(2)}) copy-start(bf16[1,8,512,512]{3,2,1,0:T(8,128)(2,1)} %param.1) | copy-start | bytes 12582916

commit v2 on v1

--- a/solution.py
+++ b/solution.py
@@ -163,32 +163,25 @@
             total = total + zin[ch, k - 1]
         img[:, :, ch * CW:(ch + 1) * CW] = total * scale
 
-    both = ((0,), (1,))
-    for g in range(2):
-        raw_relay(g, 0)
-    for g in range(2):
-        raw_pair(g, 0)
-    for g in range(2):
-        raw_direct(g, 0)
-    for ch in range(1, NCH):
-        for g in range(2):
-            raw_relay(g, ch)
-        for g in range(2):
-            raw_pair(g, ch)
-    for ch in range(NCH):
-        for g in range(2):
-            combine(g, ch)
-        if ch + 1 < NCH:
+    def each(fn, ch):
+        if 0 <= ch < NCH:
             for g in range(2):
-                raw_direct(g, ch + 1)
-        for g in range(2):
-            first_sum(g, ch)
-            second_raw(g, ch)
-        for g in range(2):
-            second_combine(g, ch)
-        for g in range(2):
-            second_sum(g, ch)
-        third_send(ch)
+                fn(g, ch)
+
+    each(raw_relay, 0)
+    each(raw_pair, 0)
+    each(raw_direct, 0)
+    for k in range(1, NCH + 5):
+        each(raw_relay, k)
+        each(raw_pair, k)
+        each(combine, k - 1)
+        each(raw_direct, k)
+        each(first_sum, k - 2)
+        each(second_raw, k - 2)
+        each(second_combine, k - 3)
+        each(second_sum, k - 4)
+        if 0 <= k - 4 < NCH:
+            third_send(k - 4)
     for ch in range(NCH):
         third_sum(ch)
 

time: 59.6 us -> 51.4 us (0.86)
  the two profiles are of different devices: /device:TPU:2 before, /device:TPU:1 now
where the time goes in v2:
time: 51.4 us; the launch traced here: 50.4 us
  Pallas kernels  47.6 us (93%)
  local copies, waits for them, and re-layouts  2.8 us (5%)
    pallas_call x1, Pallas kernels, step(): pl.pallas_call(functools.partial(kernel, scale), out_shape=jax.ShapeDtype...  47.6 us
    unnamed x3, local copies, waits for them, and re-layouts  2.8 us

profile of v2, /device:TPU:1, one launch (start us, length us, event | category | flops | bytes accessed | tf_op | source)
XLA Modules:
  0.0 50.4 jit_solution(1095321433037209990)
XLA Ops:
  0.0 0.0 copy-start
  0.0 2.2 %copy-done = bf16[1,8,512,512]{3,2,1,0:T(8,128)(2,1)S(1)} copy-done((bf16[1,8,512,512]{3,2,1,0:T(8,128)(2,1)S(1)}, bf16[1,8,512,512]{3,2,1,0:T(8,128)(2,1)}, u32[]{:S(2)}) %copy-start) | copy-done | bytes 4194328
  2.2 47.6 %shard_map.17 = f32[2,8,512]{2,1,0:T(8,128)S(1)} custom-call(bf16[8,64,8,512]{3,2,1,0:T(8,128)(2,1)S(1)} %bitcast.2, bf16[8,16,4,8,512]{4,3,2,1,0:T(8,128)(2,1)S(1)} %bitcast.3), custom_call_target="tpu_custom_call" | custom-call | tf_op jit(solution)/shard_map/pallas_call | solution.py:225
  49.8 0.6 %copy.3 = f32[2,8,512]{2,1,0:T(8,128)} copy(f32[2,8,512]{2,1,0:T(8,128)S(1)} %shard_map.17) | data formatting | bytes 65536
Async XLA Ops:
  0.0 2.2 %copy-start = (bf16[1,8,512,512]{3,2,1,0:T(8,128)(2,1)S(1)}, bf16[1,8,512,512]{3,2,1,0:T(8,128)(2,1)}, u32[]{:S(2)}) copy-start(bf16[1,8,512,512]{3,2,1,0:T(8,128)(2,1)} %param.1) | copy-start | bytes 12582916

commit v3 on v0

v3 whole, which is shorter than its diff:
```python
import functools

import jax
import jax.numpy as jnp
from jax import lax
from jax.experimental import pallas as pl
from jax.experimental.pallas import tpu as pltpu
from jax.sharding import PartitionSpec as P

MESH = pl.DeviceIdType.MESH
NCH = 4
NY = 512
CW = NY // NCH
F32 = jnp.float32
BF16 = jnp.bfloat16


def kernel(scale, pin, out, give, mine, theirs, psum, L, rel, dirt, cin, S, qrel, qdir, qin, T, zin,
           give_sem, mine_sem, th_s, th_r, rel_s, rel_r, dir_s, dir_r, c_s, c_r, qrel_s, qrel_r, qdir_s, qdir_r,
           qc_s, qc_r, z_s, z_r):
    s, t = lax.axis_index("shot"), lax.axis_index("tile")
    core, xl = lax.rem(s, 2), s // 2
    xh, z, y = t // 32, lax.rem(t // 4, 8), lax.rem(t, 4)
    X = xh * 2 + xl
    other = 1 - core
    zhalf = z // 4

    def at(Xq, zq, yq, cq):
        return (lax.rem(Xq, 2) * 2 + cq, (Xq // 2) * 32 + zq * 4 + yq)

    def wrap(v, n):
        return lax.rem(v + n, n)

    def pos(g, step):
        return wrap((X if g == 0 else y) + step, 4)

    def peer(g, step):
        return at(pos(0, step), z, y, core) if g == 0 else at(X, z, pos(1, step), core)

    sibling = at(X, z, y, other)

    def load(ch, half, dst, sem):
        cols = pl.ds(ch * CW, CW)
        for q in range(2):
            base = q * 32 + half * 16
            pltpu.make_async_copy(pin.at[:, pl.ds(base, 16), :, cols], dst.at[ch, :, q, pl.ds(1, 16)], sem.at[ch]).start()
            low = jnp.maximum(base - 1, 0)
            pltpu.make_async_copy(pin.at[:, pl.ds(low, 1), :, cols], dst.at[ch, :, q, pl.ds(0, 1)], sem.at[ch]).start()
            high = jnp.minimum(base + 16, 63)
            pltpu.make_async_copy(pin.at[:, pl.ds(high, 1), :, cols], dst.at[ch, :, q, pl.ds(17, 1)], sem.at[ch]).start()

    for ch in range(NCH):
        load(ch, other, give, give_sem)
        load(ch, core, mine, mine_sem)

    barrier = pltpu.get_barrier_semaphore()
    for dev in (sibling, peer(0, 1), peer(0, -1), peer(1, 1), peer(1, -1)):
        pl.semaphore_signal(barrier, inc=1, device_id=dev, device_id_type=MESH)
    for zq in range(8):
        @pl.when(jnp.logical_or(zhalf != core, zq != z))
        def _():
            pl.semaphore_signal(barrier, inc=1, device_id=at(X, zq, y, zhalf), device_id_type=MESH)
    for ch in range(NCH):
        for q in range(2):
            psum[ch, 0, q] = jnp.zeros((18, 8, CW), F32)
            psum[ch, 9, q] = jnp.zeros((18, 8, CW), F32)
    pl.semaphore_wait(barrier, 13 - jnp.where(zhalf == core, 1, 0))

    sends = []

    def send(src, dst, ss, rs, dev):
        cp = pltpu.make_async_remote_copy(src_ref=src, dst_ref=dst, send_sem=ss, recv_sem=rs, device_id=dev,
                                          device_id_type=MESH)
        cp.start()
        sends.append(cp)

    def wait_in(dst, rs):
        pltpu.make_async_copy(dst, dst, rs).wait()

    for ch in range(NCH):
        wait_in(give.at[ch], give_sem.at[ch])
        send(give.at[ch], theirs.at[ch], th_s.at[ch], th_r.at[ch], sibling)

    first = jnp.where(core == 0, 0.0, 1.0).astype(F32)
    last = jnp.where(core == 1, 0.0, 1.0).astype(F32)
    lane = lax.broadcasted_iota(jnp.int32, (64, CW), 1)

    def pair(ch):
        if not 0 <= ch < NCH:
            return
        wait_in(mine.at[ch], mine_sem.at[ch])
        wait_in(theirs.at[ch], th_r.at[ch])

        @pl.loop(0, 8)
        def _(d):
            for q in range(2):
                psum[ch, d + 1, q] = mine[ch, d, q].astype(F32) + theirs[ch, d, q].astype(F32)
            psum[ch, d + 1, 0, 0] = psum[ch, d + 1, 0, 0] * first
            psum[ch, d + 1, 1, 17] = psum[ch, d + 1, 1, 17] * last

    def stencil(ch, g):
        @pl.loop(0, 16)
        def _(i):
            q, xq, hf = i // 4, lax.rem(i // 2, 2), lax.rem(i, 2)
            d = 2 * q + g + 1
            mid = pl.ds(hf * 8 + 1, 8)
            w = psum[ch, d, xq, pl.ds(hf * 8, 10)].reshape(80, CW)
            c = w[8:72]
            n = (w[7:71] + w[9:73]) + (psum[ch, d - 1, xq, mid] + psum[ch, d + 1, xq, mid]).reshape(64, CW)
            before = pltpu.roll(psum[ch - 1, d, xq, mid].reshape(64, CW), 1, 1) if ch > 0 else 0.0
            after = pltpu.roll(psum[ch + 1, d, xq, mid].reshape(64, CW), CW - 1, 1) if ch < NCH - 1 else 0.0
            n = n + (jnp.where(lane == 0, before, pltpu.roll(c, 1, 1)) +
                     jnp.where(lane == CW - 1, after, pltpu.roll(c, CW - 1, 1)))
            r = (6.0 * c - n).reshape(8, 8, CW)
            if g == 0:
                L[0, ch, xq * 2 + q // 2, lax.rem(q, 2), pl.ds(hf * 8, 8)] = r
            else:
                for j in range(8):
                    L[1, ch, j % 4, lax.rem(q, 2), (q // 2) * 8 + xq * 4 + hf * 2 + j // 4] = r[j]

    DIRS = tuple(enumerate((1, -1)))

    def relay(g, ch):
        for d, step in DIRS:
            send(L.at[g, ch, pos(g, 2), d], rel.at[g, ch, d], rel_s.at[g, ch, d], rel_r.at[g, ch, d], peer(g, step))

    def direct(g, ch):
        for d, step in DIRS:
            send(L.at[g, ch, pos(g, step), 1 - d], dirt.at[g, ch, d], dir_s.at[g, ch, d], dir_r.at[g, ch, d],
                 peer(g, step))

    def combine(g, ch):
        for d, step in DIRS:
            wait_in(rel.at[g, ch, d], rel_r.at[g, ch, d])
            rel[g, ch, d] = rel[g, ch, d] + L[g, ch, pos(g, step), d]
            send(rel.at[g, ch, d], cin.at[g, ch, d], c_s.at[g, ch, d], c_r.at[g, ch, d], peer(g, step))

    def first_sum(g, ch):
        for h in range(2):
            wait_in(dirt.at[g, ch, 1 - h], dir_r.at[g, ch, 1 - h])
            wait_in(cin.at[g, ch, h], c_r.at[g, ch, h])
            total = (L[g, ch, pos(g, 0), h] + dirt[g, ch, 1 - h]) + cin[g, ch, h]
            for j in range(16):
                if g == 0:
                    S[g, ch, j % 4, h, j // 4] = total[j]
                else:
                    S[g, ch, (j // 4 % 2) * 2 + j // 8, h, j % 4] = total[j]

    def second_send(g, ch):
        o = 1 - g
        for d, step in DIRS:
            send(S.at[g, ch, pos(o, 2), d], qrel.at[g, ch, d], qrel_s.at[g, ch, d], qrel_r.at[g, ch, d], peer(o, step))
        for d, step in DIRS:
            send(S.at[g, ch, pos(o, step), 1 - d], qdir.at[g, ch, d], qdir_s.at[g, ch, d], qdir_r.at[g, ch, d],
                 peer(o, step))

    def second_combine(g, ch):
        o = 1 - g
        for d, step in DIRS:
            wait_in(qrel.at[g, ch, d], qrel_r.at[g, ch, d])
            qrel[g, ch, d] = qrel[g, ch, d] + S[g, ch, pos(o, step), d]
            send(qrel.at[g, ch, d], qin.at[g, ch, d], qc_s.at[g, ch, d], qc_r.at[g, ch, d], peer(o, step))

    def second_sum(g, ch):
        for h in range(2):
            wait_in(qdir.at[g, ch, 1 - h], qdir_r.at[g, ch, 1 - h])
            wait_in(qin.at[g, ch, h], qc_r.at[g, ch, h])
            total = (S[g, ch, pos(1 - g, 0), h] + qdir[g, ch, 1 - h]) + qin[g, ch, h]
            for j in range(4):
                T[ch, h, j, g] = total[j]

    zsends = []

    def third_send(ch):
        for k in range(4):
            j = lax.rem(z + k, 4)
            zq = core * 4 + j
            for cq in range(2):
                cp = pltpu.make_async_remote_copy(
                    src_ref=T.at[ch, cq, j], dst_ref=zin.at[ch, z], send_sem=z_s.at[ch, j, cq],
                    recv_sem=z_r.at[ch, z], device_id=at(X, zq, y, cq), device_id_type=MESH)
                remote = jnp.logical_or(zq != z, core != cq)
                zsends.append((cp, remote))

                @pl.when(remote)
                def _():
                    cp.start()

                @pl.when(jnp.logical_not(remote))
                def _():
                    zin[ch, z] = T[ch, cq, j]

    def third_sum(ch):
        for k in range(8):
            @pl.when(jnp.logical_or(zhalf != core, k != z))
            def _():
                wait_in(zin.at[ch, k], z_r.at[ch, k])
        total = (zin[ch, 0] + zin[ch, 1]) + (zin[ch, 2] + zin[ch, 3])
        total = total + ((zin[ch, 4] + zin[ch, 5]) + (zin[ch, 6] + zin[ch, 7]))
        out[:, :, ch * CW:(ch + 1) * CW] = total * scale

    def each(fn, ch):
        if 0 <= ch < NCH:
            for g in range(2):
                fn(g, ch)

    pair(0)
    for k in range(NCH + 4):
        pair(k + 1)
        if k < NCH:
            for g in range(2):
                stencil(k, g)
                relay(g, k)
        each(combine, k - 1)
        each(direct, k)
        each(first_sum, k - 2)
        each(second_send, k - 2)
        each(second_combine, k - 3)
        each(second_sum, k - 4)
        if 0 <= k - 4 < NCH:
            third_send(k - 4)
    for ch in range(NCH):
        third_sum(ch)
    for cp in sends:
        cp.wait_send()
    for cp, remote in zsends:
        @pl.when(remote)
        def _():
            cp.wait_send()


def solution(mesh):
    shots = mesh.shape["shot"] * mesh.shape["tile"]
    scale = 1.0 / float(shots) ** 0.5
    D = pltpu.SemaphoreType.DMA
    V = pltpu.VMEM

    def step(partials):
        return pl.pallas_call(
            functools.partial(kernel, scale),
            out_shape=jax.ShapeDtypeStruct((2, 8, NY), F32),
            in_specs=[pl.BlockSpec(memory_space=pl.ANY)],
            out_specs=pl.BlockSpec(memory_space=pltpu.VMEM),
            scratch_shapes=[
                V((NCH, 8, 2, 18, 8, CW), BF16),
                V((NCH, 8, 2, 18, 8, CW), BF16),
                V((NCH, 8, 2, 18, 8, CW), BF16),
                V((NCH, 10, 2, 18, 8, CW), F32),
                V((2, NCH, 4, 2, 16, 8, CW), F32),
                V((2, NCH, 2, 16, 8, CW), F32),
                V((2, NCH, 2, 16, 8, CW), F32),
                V((2, NCH, 2, 16, 8, CW), F32),
                V((2, NCH, 4, 2, 4, 8, CW), F32),
                V((2, NCH, 2, 4, 8, CW), F32),
                V((2, NCH, 2, 4, 8, CW), F32),
                V((2, NCH, 2, 4, 8, CW), F32),
                V((NCH, 2, 4, 2, 8, CW), F32),
                V((NCH, 8, 2, 8, CW), F32),
                D((NCH,)), D((NCH,)), D((NCH,)), D((NCH,)),
                D((2, NCH, 2)), D((2, NCH, 2)),
                D((2, NCH, 2)), D((2, NCH, 2)),
                D((2, NCH, 2)), D((2, NCH, 2)),
                D((2, NCH, 2)), D((2, NCH, 2)),
                D((2, NCH, 2)), D((2, NCH, 2)),
                D((2, NCH, 2)), D((2, NCH, 2)),
                D((NCH, 4, 2)), D((NCH, 8)),
            ],
            compiler_params=pltpu.CompilerParams(collective_id=0, has_side_effects=True,
                                                 vmem_limit_bytes=62 * 1024 * 1024),
        )(partials.reshape(8, 64, 8, NY))

    return jax.shard_map(step, mesh=mesh, in_specs=(P(("shot", "tile"), None, None, None),),
                         out_specs=P("shot", "tile", None), check_vma=False)
```

time: 152 us -> 54.5 us (0.36)
  the two profiles are of different devices: /device:TPU:6 before, /device:TPU:1 now
where the time goes in v3:
time: 54.5 us; the launch traced here: 54.4 us
  Pallas kernels  53 us (97%)
  local copies, waits for them, and re-layouts  1.38 us (3%)
    pallas_call x1, Pallas kernels, step(): pl.pallas_call(functools.partial(kernel, scale), out_shape=jax.ShapeDtype...  53 us
    unnamed x1, local copies, waits for them, and re-layouts  1.38 us

profile of v3, /device:TPU:1, one launch (start us, length us, event | category | flops | bytes accessed | tf_op | source)
XLA Modules:
  0.0 54.4 jit_solution(11188606901536642829)
XLA Ops:
  0.0 53.0 %shard_map.17 = f32[2,8,512]{2,1,0:T(8,128)} custom-call(bf16[8,64,8,512]{3,2,1,0:T(8,128)(2,1)} %bitcast.1), custom_call_target="tpu_custom_call" | custom-call | tf_op jit(solution)/shard_map/pallas_call | solution.py:239
  53.0 1.4 %copy.3 = f32[2,8,512]{2,1,0:T(8,128)} copy(f32[2,8,512]{2,1,0:T(8,128)} %shard_map.17) | data formatting | bytes 65536

commit v4 on v3

--- a/solution.py
+++ b/solution.py
@@ -11,13 +11,15 @@
 NCH = 4
 NY = 512
 CW = NY // NCH
+UNROLL = 2
+STRAIGHT = (3,)
 F32 = jnp.float32
 BF16 = jnp.bfloat16
 
 
-def kernel(scale, pin, out, give, mine, theirs, psum, L, rel, dirt, cin, S, qrel, qdir, qin, T, zin,
+def kernel(scale, pin, out, give, mine, theirs, psum, L, rel, dirt, cin, S, qrel, qdir, qin, qall, T, zin,
            give_sem, mine_sem, th_s, th_r, rel_s, rel_r, dir_s, dir_r, c_s, c_r, qrel_s, qrel_r, qdir_s, qdir_r,
-           qc_s, qc_r, z_s, z_r):
+           qc_s, qc_r, qa_s, qa_r, z_s, z_r, tok):
     s, t = lax.axis_index("shot"), lax.axis_index("tile")
     core, xl = lax.rem(s, 2), s // 2
     xh, z, y = t // 32, lax.rem(t // 4, 8), lax.rem(t, 4)
@@ -53,18 +55,26 @@
         load(ch, other, give, give_sem)
         load(ch, core, mine, mine_sem)
 
+    zring = (at(X, wrap(z + 1, 8), y, core), at(X, wrap(z - 1, 8), y, core))
     barrier = pltpu.get_barrier_semaphore()
-    for dev in (sibling, peer(0, 1), peer(0, -1), peer(1, 1), peer(1, -1)):
+    for dev in (sibling, peer(0, 1), peer(0, -1), peer(1, 1), peer(1, -1), *zring):
         pl.semaphore_signal(barrier, inc=1, device_id=dev, device_id_type=MESH)
-    for zq in range(8):
-        @pl.when(jnp.logical_or(zhalf != core, zq != z))
-        def _():
-            pl.semaphore_signal(barrier, inc=1, device_id=at(X, zq, y, zhalf), device_id_type=MESH)
     for ch in range(NCH):
         for q in range(2):
-            psum[ch, 0, q] = jnp.zeros((18, 8, CW), F32)
-            psum[ch, 9, q] = jnp.zeros((18, 8, CW), F32)
-    pl.semaphore_wait(barrier, 13 - jnp.where(zhalf == core, 1, 0))
+            psum[ch, 0, q] = jnp.zeros((144, CW), F32)
+            psum[ch, 9, q] = jnp.zeros((144, CW), F32)
+    pl.semaphore_wait(barrier, 7)
+
+    def token(k, devices):
+        for dev in devices:
+            pl.semaphore_signal(tok.at[k], inc=1, device_id=dev, device_id_type=MESH)
+
+    def pass_token(k):
+        pl.semaphore_wait(tok.at[k], 2 if k < 3 else 1)
+        if k < 3:
+            token(k + 1, zring if k < 2 else (sibling,))
+
+    token(0, zring)
 
     sends = []
 
@@ -94,29 +104,31 @@
         @pl.loop(0, 8)
         def _(d):
             for q in range(2):
-                psum[ch, d + 1, q] = mine[ch, d, q].astype(F32) + theirs[ch, d, q].astype(F32)
-            psum[ch, d + 1, 0, 0] = psum[ch, d + 1, 0, 0] * first
-            psum[ch, d + 1, 1, 17] = psum[ch, d + 1, 1, 17] * last
+                psum[ch, d + 1, q] = (mine[ch, d, q].astype(F32) + theirs[ch, d, q].astype(F32)).reshape(144, CW)
+            psum[ch, d + 1, 0, 0:8] = psum[ch, d + 1, 0, 0:8] * first
+            psum[ch, d + 1, 1, 136:144] = psum[ch, d + 1, 1, 136:144] * last
 
     def stencil(ch, g):
-        @pl.loop(0, 16)
+        @pl.loop(0, 8, unroll=UNROLL)
         def _(i):
-            q, xq, hf = i // 4, lax.rem(i // 2, 2), lax.rem(i, 2)
+            q, xq = i // 2, lax.rem(i, 2)
             d = 2 * q + g + 1
-            mid = pl.ds(hf * 8 + 1, 8)
-            w = psum[ch, d, xq, pl.ds(hf * 8, 10)].reshape(80, CW)
-            c = w[8:72]
-            n = (w[7:71] + w[9:73]) + (psum[ch, d - 1, xq, mid] + psum[ch, d + 1, xq, mid]).reshape(64, CW)
-            before = pltpu.roll(psum[ch - 1, d, xq, mid].reshape(64, CW), 1, 1) if ch > 0 else 0.0
-            after = pltpu.roll(psum[ch + 1, d, xq, mid].reshape(64, CW), CW - 1, 1) if ch < NCH - 1 else 0.0
-            n = n + (jnp.where(lane == 0, before, pltpu.roll(c, 1, 1)) +
-                     jnp.where(lane == CW - 1, after, pltpu.roll(c, CW - 1, 1)))
-            r = (6.0 * c - n).reshape(8, 8, CW)
-            if g == 0:
-                L[0, ch, xq * 2 + q // 2, lax.rem(q, 2), pl.ds(hf * 8, 8)] = r
-            else:
-                for j in range(8):
-                    L[1, ch, j % 4, lax.rem(q, 2), (q // 2) * 8 + xq * 4 + hf * 2 + j // 4] = r[j]
+            for hf in range(2):
+                lo = hf * 64 + 8
+                mid = slice(lo, lo + 64)
+                c = psum[ch, d, xq, mid]
+                before = psum[ch - 1, d, xq, mid] if ch > 0 else 0.0
+                after = psum[ch + 1, d, xq, mid] if ch < NCH - 1 else 0.0
+                n = psum[ch, d, xq, slice(lo - 1, lo + 63)] + psum[ch, d, xq, slice(lo + 1, lo + 65)]
+                n = n + (psum[ch, d - 1, xq, mid] + psum[ch, d + 1, xq, mid])
+                n = n + (pltpu.roll(jnp.where(lane == CW - 1, before, c), 1, 1) +
+                         pltpu.roll(jnp.where(lane == 0, after, c), CW - 1, 1))
+                r = (6.0 * c - n).reshape(8, 8, CW)
+                if g == 0:
+                    L[0, ch, xq * 2 + q // 2, lax.rem(q, 2), pl.ds(hf * 8, 8)] = r
+                else:
+                    for j in range(8):
+                        L[1, ch, j % 4, lax.rem(q, 2), (q // 2) * 8 + xq * 4 + hf * 2 + j // 4] = r[j]
 
     DIRS = tuple(enumerate((1, -1)))
 
@@ -148,6 +160,10 @@
 
     def second_send(g, ch):
         o = 1 - g
+        if ch in STRAIGHT:
+            for j, step in enumerate((2, 1, -1)):
+                send(S.at[g, ch, pos(o, step)], qall.at[g, ch, j], qa_s.at[g, ch, j], qa_r.at[g, ch, j], peer(o, step))
+            return
         for d, step in DIRS:
             send(S.at[g, ch, pos(o, 2), d], qrel.at[g, ch, d], qrel_s.at[g, ch, d], qrel_r.at[g, ch, d], peer(o, step))
         for d, step in DIRS:
@@ -156,12 +172,22 @@
 
     def second_combine(g, ch):
         o = 1 - g
+        if ch in STRAIGHT:
+            return
         for d, step in DIRS:
             wait_in(qrel.at[g, ch, d], qrel_r.at[g, ch, d])
             qrel[g, ch, d] = qrel[g, ch, d] + S[g, ch, pos(o, step), d]
             send(qrel.at[g, ch, d], qin.at[g, ch, d], qc_s.at[g, ch, d], qc_r.at[g, ch, d], peer(o, step))
 
     def second_sum(g, ch):
+        if ch in STRAIGHT:
+            for j in range(3):
+                wait_in(qall.at[g, ch, j], qa_r.at[g, ch, j])
+            total = (S[g, ch, pos(1 - g, 0)] + qall[g, ch, 0]) + (qall[g, ch, 1] + qall[g, ch, 2])
+            for h in range(2):
+                for j in range(4):
+                    T[ch, h, j, g] = total[h, j]
+            return
         for h in range(2):
             wait_in(qdir.at[g, ch, 1 - h], qdir_r.at[g, ch, 1 - h])
             wait_in(qin.at[g, ch, h], qc_r.at[g, ch, h])
@@ -217,6 +243,8 @@
         each(second_send, k - 2)
         each(second_combine, k - 3)
         each(second_sum, k - 4)
+        if 1 <= k < 5:
+            pass_token(k - 1)
         if 0 <= k - 4 < NCH:
             third_send(k - 4)
     for ch in range(NCH):
@@ -245,7 +273,7 @@
                 V((NCH, 8, 2, 18, 8, CW), BF16),
                 V((NCH, 8, 2, 18, 8, CW), BF16),
                 V((NCH, 8, 2, 18, 8, CW), BF16),
-                V((NCH, 10, 2, 18, 8, CW), F32),
+                V((NCH, 10, 2, 144, CW), F32),
                 V((2, NCH, 4, 2, 16, 8, CW), F32),
                 V((2, NCH, 2, 16, 8, CW), F32),
                 V((2, NCH, 2, 16, 8, CW), F32),
@@ -254,6 +282,7 @@
                 V((2, NCH, 2, 4, 8, CW), F32),
                 V((2, NCH, 2, 4, 8, CW), F32),
                 V((2, NCH, 2, 4, 8, CW), F32),
+                V((2, NCH, 3, 2, 4, 8, CW), F32),
                 V((NCH, 2, 4, 2, 8, CW), F32),
                 V((NCH, 8, 2, 8, CW), F32),
                 D((NCH,)), D((NCH,)), D((NCH,)), D((NCH,)),
@@ -263,10 +292,12 @@
                 D((2, NCH, 2)), D((2, NCH, 2)),
                 D((2, NCH, 2)), D((2, NCH, 2)),
                 D((2, NCH, 2)), D((2, NCH, 2)),
+                D((2, NCH, 3)), D((2, NCH, 3)),
                 D((NCH, 4, 2)), D((NCH, 8)),
+                pltpu.SemaphoreType.REGULAR((4,)),
             ],
             compiler_params=pltpu.CompilerParams(collective_id=0, has_side_effects=True,
-                                                 vmem_limit_bytes=62 * 1024 * 1024),
+                                                 vmem_limit_bytes=52 * 1024 * 1024),
         )(partials.reshape(8, 64, 8, NY))
 
     return jax.shard_map(step, mesh=mesh, in_specs=(P(("shot", "tile"), None, None, None),),

time: 54.5 us -> 48.4 us (0.89)
  Pallas kernels: 53 us -> 47.7 us
  local copies, waits for them, and re-layouts: 1.38 us -> 0.62 us
    pallas_call x1, Pallas kernels: 53 us -> 47.7 us  [step(): pl.pallas_call(functools.partial(kernel, scale), out_shape=jax.ShapeDtype...]
    unnamed x1, local copies, waits for them, and re-layouts: 1.38 us -> 0.62 us
where the time goes in v4:
time: 48.4 us; the launch traced here: 48.3 us
  Pallas kernels  47.7 us (99%)
  local copies, waits for them, and re-layouts  0.62 us (1%)
    pallas_call x1, Pallas kernels, step(): pl.pallas_call(functools.partial(kernel, scale), out_shape=jax.ShapeDtype...  47.7 us

profile of v4, /device:TPU:1, one launch (start us, length us, event | category | flops | bytes accessed | tf_op | source)
XLA Modules:
  0.0 48.3 jit_solution(17309811489972631976)
XLA Ops:
  0.0 47.7 %shard_map.17 = f32[2,8,512]{2,1,0:T(8,128)S(1)} custom-call(bf16[8,64,8,512]{3,2,1,0:T(8,128)(2,1)} %bitcast.1), custom_call_target="tpu_custom_call" | custom-call | tf_op jit(solution)/shard_map/pallas_call | solution.py:267
  47.7 0.6 %copy.3 = f32[2,8,512]{2,1,0:T(8,128)} copy(f32[2,8,512]{2,1,0:T(8,128)S(1)} %shard_map.17) | data formatting | bytes 65536

commit v5 on v4

--- a/solution.py
+++ b/solution.py
@@ -8,18 +8,21 @@
 from jax.sharding import PartitionSpec as P
 
 MESH = pl.DeviceIdType.MESH
-NCH = 4
 NY = 512
-CW = NY // NCH
+CW = 128
+NT = NY // CW
+TILES = (0, 2, 3)
+ZTILE = 1
+NCH = len(TILES)
 UNROLL = 2
-STRAIGHT = (3,)
+STRAIGHT = (2,)
 F32 = jnp.float32
 BF16 = jnp.bfloat16
 
 
-def kernel(scale, pin, out, give, mine, theirs, psum, L, rel, dirt, cin, S, qrel, qdir, qin, qall, T, zin,
+def kernel(scale, pin, out, give, mine, theirs, psum, L, rel, dirt, cin, S, qrel, qdir, qin, qall, T, zin, LC, zc, R, xyin,
            give_sem, mine_sem, th_s, th_r, rel_s, rel_r, dir_s, dir_r, c_s, c_r, qrel_s, qrel_r, qdir_s, qdir_r,
-           qc_s, qc_r, qa_s, qa_r, z_s, z_r, tok):
+           qc_s, qc_r, qa_s, qa_r, z_s, z_r, zc_s, zc_r, xy_s, xy_r, tok):
     s, t = lax.axis_index("shot"), lax.axis_index("tile")
     core, xl = lax.rem(s, 2), s // 2
     xh, z, y = t // 32, lax.rem(t // 4, 8), lax.rem(t, 4)
@@ -51,7 +54,7 @@
             high = jnp.minimum(base + 16, 63)
             pltpu.make_async_copy(pin.at[:, pl.ds(high, 1), :, cols], dst.at[ch, :, q, pl.ds(17, 1)], sem.at[ch]).start()
 
-    for ch in range(NCH):
+    for ch in range(NT):
         load(ch, other, give, give_sem)
         load(ch, core, mine, mine_sem)
 
@@ -59,7 +62,7 @@
     barrier = pltpu.get_barrier_semaphore()
     for dev in (sibling, peer(0, 1), peer(0, -1), peer(1, 1), peer(1, -1), *zring):
         pl.semaphore_signal(barrier, inc=1, device_id=dev, device_id_type=MESH)
-    for ch in range(NCH):
+    for ch in range(NT):
         for q in range(2):
             psum[ch, 0, q] = jnp.zeros((144, CW), F32)
             psum[ch, 9, q] = jnp.zeros((144, CW), F32)
@@ -87,7 +90,7 @@
     def wait_in(dst, rs):
         pltpu.make_async_copy(dst, dst, rs).wait()
 
-    for ch in range(NCH):
+    for ch in range(NT):
         wait_in(give.at[ch], give_sem.at[ch])
         send(give.at[ch], theirs.at[ch], th_s.at[ch], th_r.at[ch], sibling)
 
@@ -96,8 +99,6 @@
     lane = lax.broadcasted_iota(jnp.int32, (64, CW), 1)
 
     def pair(ch):
-        if not 0 <= ch < NCH:
-            return
         wait_in(mine.at[ch], mine_sem.at[ch])
         wait_in(theirs.at[ch], th_r.at[ch])
 
@@ -108,7 +109,9 @@
             psum[ch, d + 1, 0, 0:8] = psum[ch, d + 1, 0, 0:8] * first
             psum[ch, d + 1, 1, 136:144] = psum[ch, d + 1, 1, 136:144] * last
 
-    def stencil(ch, g):
+    def stencil(tile, g):
+        ch = TILES.index(tile) if tile != ZTILE else None
+
         @pl.loop(0, 8, unroll=UNROLL)
         def _(i):
             q, xq = i // 2, lax.rem(i, 2)
@@ -116,15 +119,18 @@
             for hf in range(2):
                 lo = hf * 64 + 8
                 mid = slice(lo, lo + 64)
-                c = psum[ch, d, xq, mid]
-                before = psum[ch - 1, d, xq, mid] if ch > 0 else 0.0
-                after = psum[ch + 1, d, xq, mid] if ch < NCH - 1 else 0.0
-                n = psum[ch, d, xq, slice(lo - 1, lo + 63)] + psum[ch, d, xq, slice(lo + 1, lo + 65)]
-                n = n + (psum[ch, d - 1, xq, mid] + psum[ch, d + 1, xq, mid])
+                c = psum[tile, d, xq, mid]
+                before = psum[tile - 1, d, xq, mid] if tile > 0 else 0.0
+                after = psum[tile + 1, d, xq, mid] if tile < NT - 1 else 0.0
+                n = psum[tile, d, xq, slice(lo - 1, lo + 63)] + psum[tile, d, xq, slice(lo + 1, lo + 65)]
+                n = n + (psum[tile, d - 1, xq, mid] + psum[tile, d + 1, xq, mid])
                 n = n + (pltpu.roll(jnp.where(lane == CW - 1, before, c), 1, 1) +
                          pltpu.roll(jnp.where(lane == 0, after, c), CW - 1, 1))
                 r = (6.0 * c - n).reshape(8, 8, CW)
-                if g == 0:
+                if tile == ZTILE:
+                    for j in range(8):
+                        LC[g, hf * 2 + j // 4, lax.rem(q, 2), (q // 2) * 8 + xq * 4 + j % 4] = r[j]
+                elif g == 0:
                     L[0, ch, xq * 2 + q // 2, lax.rem(q, 2), pl.ds(hf * 8, 8)] = r
                 else:
                     for j in range(8):
@@ -223,32 +229,126 @@
                 wait_in(zin.at[ch, k], z_r.at[ch, k])
         total = (zin[ch, 0] + zin[ch, 1]) + (zin[ch, 2] + zin[ch, 3])
         total = total + ((zin[ch, 4] + zin[ch, 5]) + (zin[ch, 6] + zin[ch, 7]))
-        out[:, :, ch * CW:(ch + 1) * CW] = total * scale
+        out[:, :, TILES[ch] * CW:(TILES[ch] + 1) * CW] = total * scale
+
+    def send_if(cond, src, dst, ss, rs, dev):
+        cp = pltpu.make_async_remote_copy(src_ref=src, dst_ref=dst, send_sem=ss, recv_sem=rs, device_id=dev,
+                                          device_id_type=MESH)
+        zsends.append((cp, cond))
+
+        @pl.when(cond)
+        def _():
+            cp.start()
+
+    def z_stage(j):
+        for g in range(2):
+            for d, step in DIRS:
+                dest = wrap(z + step * (5 - j), 8)
+                active = dest // 4 == core
+                block = lax.rem(dest, 4)
+                if j == 1:
+                    send_if(active, LC.at[g, block, d], zc.at[d, 0, g, d], zc_s.at[d, 0, g], zc_r.at[d, 0, g], zring[d])
+                    continue
+
+                @pl.when(active)
+                def _():
+                    if j == 2:
+                        wait_in(zc.at[d, 0, g, d], zc_r.at[d, 0, g])
+                        LC[g, block, d] = LC[g, block, d] + zc[d, 0, g, d]
+                    else:
+                        wait_in(zc.at[d, j - 2, g], zc_r.at[d, j - 2, g])
+                        LC[g, block] = LC[g, block] + zc[d, j - 2, g]
+
+                send_if(active, LC.at[g, block], zc.at[d, j - 1, g], zc_s.at[d, j - 1, g], zc_r.at[d, j - 1, g], zring[d])
+
+    holds = zhalf == core
+    me = X * 4 + y
+
+    def z_final():
+        block = lax.rem(z, 4)
+
+        @pl.when(holds)
+        def _():
+            for g in range(2):
+                for d in range(2):
+                    wait_in(zc.at[d, 3, g], zc_r.at[d, 3, g])
+
+                @pl.loop(0, 16)
+                def _(i):
+                    for cq in range(2):
+                        R[cq, i, g] = (LC[g, block, cq, i] + zc[0, 3, g, cq, i]) + zc[1, 3, g, cq, i]
+
+            xyin[me] = R[core, lax.rem(X, 2) * 8 + (X // 2) * 4 + y]
+
+        for a in (2, 1, 3, 0):
+            for b in (2, 1, 3, 0):
+                Xq, yq = wrap(X + a, 4), wrap(y + b, 4)
+                i = lax.rem(Xq, 2) * 8 + (Xq // 2) * 4 + yq
+                for cq in range(2):
+                    cond = holds if a or b else jnp.logical_and(holds, core != cq)
+                    send_if(cond, R.at[cq, i], xyin.at[me], xy_s.at[a, b, cq], xy_r.at[me], at(Xq, z, yq, cq))
+
+    def xy_sum():
+        for k in range(16):
+            @pl.when(jnp.logical_or(jnp.logical_not(holds), k != me))
+            def _():
+                wait_in(xyin.at[k], xy_r.at[k])
+        parts = [xyin[k] for k in range(16)]
+        while len(parts) > 1:
+            parts = [parts[k] + parts[k + 1] for k in range(0, len(parts), 2)]
+        out[:, :, ZTILE * CW:(ZTILE + 1) * CW] = parts[0] * scale
 
     def each(fn, ch):
-        if 0 <= ch < NCH:
-            for g in range(2):
-                fn(g, ch)
+        for g in range(2):
+            fn(g, ch)
+
+    def begin(ch):
+        for g in range(2):
+            stencil(TILES[ch], g)
+            relay(g, ch)
 
     pair(0)
-    for k in range(NCH + 4):
-        pair(k + 1)
-        if k < NCH:
-            for g in range(2):
-                stencil(k, g)
-                relay(g, k)
-        each(combine, k - 1)
-        each(direct, k)
-        each(first_sum, k - 2)
-        each(second_send, k - 2)
-        each(second_combine, k - 3)
-        each(second_sum, k - 4)
-        if 1 <= k < 5:
-            pass_token(k - 1)
-        if 0 <= k - 4 < NCH:
-            third_send(k - 4)
-    for ch in range(NCH):
-        third_sum(ch)
+    pair(1)
+    begin(0)
+    each(direct, 0)
+    pair(2)
+    for g in range(2):
+        stencil(ZTILE, g)
+    z_stage(1)
+    pair(3)
+    begin(1)
+    each(combine, 0)
+    each(direct, 1)
+    pass_token(0)
+    z_stage(2)
+    begin(2)
+    each(combine, 1)
+    each(direct, 2)
+    pass_token(1)
+    each(first_sum, 0)
+    each(second_send, 0)
+    z_stage(3)
+    each(combine, 2)
+    pass_token(2)
+    each(first_sum, 1)
+    each(second_send, 1)
+    each(second_combine, 0)
+    z_stage(4)
+    each(first_sum, 2)
+    each(second_send, 2)
+    each(second_combine, 1)
+    each(second_sum, 0)
+    pass_token(3)
+    third_send(0)
+    each(second_sum, 1)
+    third_send(1)
+    z_final()
+    each(second_sum, 2)
+    third_send(2)
+    third_sum(0)
+    third_sum(1)
+    xy_sum()
+    third_sum(2)
     for cp in sends:
         cp.wait_send()
     for cp, remote in zsends:
@@ -270,10 +370,10 @@
             in_specs=[pl.BlockSpec(memory_space=pl.ANY)],
             out_specs=pl.BlockSpec(memory_space=pltpu.VMEM),
             scratch_shapes=[
-                V((NCH, 8, 2, 18, 8, CW), BF16),
-                V((NCH, 8, 2, 18, 8, CW), BF16),
-                V((NCH, 8, 2, 18, 8, CW), BF16),
-                V((NCH, 10, 2, 144, CW), F32),
+                V((NT, 8, 2, 18, 8, CW), BF16),
+                V((NT, 8, 2, 18, 8, CW), BF16),
+                V((NT, 8, 2, 18, 8, CW), BF16),
+                V((NT, 10, 2, 144, CW), F32),
                 V((2, NCH, 4, 2, 16, 8, CW), F32),
                 V((2, NCH, 2, 16, 8, CW), F32),
                 V((2, NCH, 2, 16, 8, CW), F32),
@@ -285,7 +385,11 @@
                 V((2, NCH, 3, 2, 4, 8, CW), F32),
                 V((NCH, 2, 4, 2, 8, CW), F32),
                 V((NCH, 8, 2, 8, CW), F32),
-                D((NCH,)), D((NCH,)), D((NCH,)), D((NCH,)),
+                V((2, 4, 2, 16, 8, CW), F32),
+                V((2, 4, 2, 2, 16, 8, CW), F32),
+                V((2, 16, 2, 8, CW), F32),
+                V((16, 2, 8, CW), F32),
+                D((NT,)), D((NT,)), D((NT,)), D((NT,)),
                 D((2, NCH, 2)), D((2, NCH, 2)),
                 D((2, NCH, 2)), D((2, NCH, 2)),
                 D((2, NCH, 2)), D((2, NCH, 2)),
@@ -294,6 +398,8 @@
                 D((2, NCH, 2)), D((2, NCH, 2)),
                 D((2, NCH, 3)), D((2, NCH, 3)),
                 D((NCH, 4, 2)), D((NCH, 8)),
+                D((2, 4, 2)), D((2, 4, 2)),
+                D((4, 4, 2)), D((16,)),
                 pltpu.SemaphoreType.REGULAR((4,)),
             ],
             compiler_params=pltpu.CompilerParams(collective_id=0, has_side_effects=True,

time: 48.4 us -> 43.4 us (0.90)
  Pallas kernels: 47.7 us -> 42.7 us
    pallas_call x1, Pallas kernels: 47.7 us -> 42.7 us  [step(): pl.pallas_call(functools.partial(kernel, scale), out_shape=jax.ShapeDtype...]
where the time goes in v5:
time: 43.4 us; the launch traced here: 43.3 us
  Pallas kernels  42.7 us (98%)
  local copies, waits for them, and re-layouts  0.62 us (1%)
    pallas_call x1, Pallas kernels, step(): pl.pallas_call(functools.partial(kernel, scale), out_shape=jax.ShapeDtype...  42.7 us

profile of v5, /device:TPU:1, one launch (start us, length us, event | category | flops | bytes accessed | tf_op | source)
XLA Modules:
  0.0 43.3 jit_solution(9607272620037068407)
XLA Ops:
  0.0 42.7 %shard_map.17 = f32[2,8,512]{2,1,0:T(8,128)S(1)} custom-call(bf16[8,64,8,512]{3,2,1,0:T(8,128)(2,1)} %bitcast.1), custom_call_target="tpu_custom_call" | custom-call | tf_op jit(solution)/shard_map/pallas_call | solution.py:367
  42.7 0.6 %copy.3 = f32[2,8,512]{2,1,0:T(8,128)} copy(f32[2,8,512]{2,1,0:T(8,128)S(1)} %shard_map.17) | data formatting | bytes 65536

commit v6 on v5

v6 whole, which is shorter than its diff:
```python
import functools

import jax
import jax.numpy as jnp
from jax import lax
from jax.experimental import pallas as pl
from jax.experimental.pallas import tpu as pltpu
from jax.sharding import PartitionSpec as P

MESH = pl.DeviceIdType.MESH
NY = 512
CW = 128
NT = NY // CW
TILES = (0, 2, 3)
ZTILE = 1
NCH = len(TILES)
UNROLL = 2
F32 = jnp.float32
BF16 = jnp.bfloat16


def kernel(scale, pin, out, give, mine, theirs, psum, L, rel, inn, S, qrel, qinn, qall, T, zin, LC, zc, R, xyin,
           give_sem, mine_sem, th_r, rel_r, in_r, qrel_r, qin_r, qall_r, z_r, zc_r, xy_r, snd, zc_s, tok):
    s, t = lax.axis_index("shot"), lax.axis_index("tile")
    core, xl = lax.rem(s, 2), s // 2
    xh, z, y = t // 32, lax.rem(t // 4, 8), lax.rem(t, 4)
    X = xh * 2 + xl
    other = 1 - core
    holds = z // 4 == core
    me = X * 4 + y
    DIRS = tuple(enumerate((1, -1)))

    def at(Xq, zq, yq, cq):
        return (lax.rem(Xq, 2) * 2 + cq, (Xq // 2) * 32 + zq * 4 + yq)

    def wrap(v, n):
        return lax.rem(v + n, n)

    def pos(g, step):
        return wrap((X if g == 0 else y) + step, 4)

    def peer(g, step):
        return at(pos(0, step), z, y, core) if g == 0 else at(X, z, pos(1, step), core)

    sibling = at(X, z, y, other)
    zring = (at(X, wrap(z + 1, 8), y, core), at(X, wrap(z - 1, 8), y, core))
    barrier = pltpu.get_barrier_semaphore()
    for dev in (sibling, peer(0, 1), peer(0, -1), peer(1, 1), peer(1, -1), *zring):
        pl.semaphore_signal(barrier, inc=1, device_id=dev, device_id_type=MESH)

    def load(tile, xq, half, dst, sem):
        cols = pl.ds(tile * CW, CW)
        base = xq * 32 + half * 16
        pltpu.make_async_copy(pin.at[:, pl.ds(base, 16), :, cols], dst.at[tile, xq, :, pl.ds(1, 16)], sem.at[tile, xq]).start()
        low = jnp.maximum(base - 1, 0)
        pltpu.make_async_copy(pin.at[:, pl.ds(low, 1), :, cols], dst.at[tile, xq, :, pl.ds(0, 1)], sem.at[tile, xq]).start()
        high = jnp.minimum(base + 16, 63)
        pltpu.make_async_copy(pin.at[:, pl.ds(high, 1), :, cols], dst.at[tile, xq, :, pl.ds(17, 1)], sem.at[tile, xq]).start()

    far, near = 1 - xh, xh
    ORDER = ((0, far), (1, far), (0, near), (1, near), (2, near), (2, far), (3, near), (3, far))

    def load_both(k):
        for tile, xq in ORDER[k:k + 2]:
            load(tile, xq, other, give, give_sem)
        for tile, xq in ORDER[k:k + 2]:
            load(tile, xq, core, mine, mine_sem)

    load_both(0)
    load_both(2)
    for tile in range(NT):
        for xq in range(2):
            psum[tile, 0, xq] = jnp.zeros((144, CW), F32)
            psum[tile, 9, xq] = jnp.zeros((144, CW), F32)
    pl.semaphore_wait(barrier, 7)

    def token(k, devices):
        for dev in devices:
            pl.semaphore_signal(tok.at[k], inc=1, device_id=dev, device_id_type=MESH)

    def pass_token(k):
        pl.semaphore_wait(tok.at[k], 2 if k < 3 else 1)
        if k < 3:
            token(k + 1, zring if k < 2 else (sibling,))

    def remote(src, dst, ss, rs, dev):
        return pltpu.make_async_remote_copy(src_ref=src, dst_ref=dst, send_sem=ss, recv_sem=rs, device_id=dev,
                                            device_id_type=MESH)

    def send(src, dst, ss, rs, dev):
        remote(src, dst, ss, rs, dev).start()

    def send_if(cond, src, dst, ss, rs, dev):
        @pl.when(cond)
        def _():
            remote(src, dst, ss, rs, dev).start()

    def wait_in(dst, rs):
        pltpu.make_async_copy(dst, dst, rs).wait()

    def hand_over(k):
        for tile, xq in ORDER[k:k + 2]:
            wait_in(give.at[tile, xq], give_sem.at[tile, xq])
            send(give.at[tile, xq], theirs.at[tile, xq], snd.at[0], th_r.at[tile, xq], sibling)

    hand_over(0)
    hand_over(2)
    load_both(4)
    load_both(6)
    token(0, zring)

    lane = lax.broadcasted_iota(jnp.int32, (64, CW), 1)

    def pair(k):
        for tile, xq in ORDER[k:k + 2]:
            wait_in(mine.at[tile, xq], mine_sem.at[tile, xq])
            wait_in(theirs.at[tile, xq], th_r.at[tile, xq])
            low = jnp.where(jnp.logical_and(core == 0, xq == 0), 0.0, 1.0).astype(F32)
            high = jnp.where(jnp.logical_and(core == 1, xq == 1), 0.0, 1.0).astype(F32)

            @pl.loop(0, 8)
            def _(d):
                v = (mine[tile, xq, d].astype(F32) + theirs[tile, xq, d].astype(F32)).reshape(144, CW)
                psum[tile, d + 1, xq, 8:136] = v[8:136]
                psum[tile, d + 1, xq, 0:8] = v[0:8] * low
                psum[tile, d + 1, xq, 136:144] = v[136:144] * high

    def stencil(tile, g, xq):
        ch = TILES.index(tile) if tile != ZTILE else None

        @pl.loop(0, 4, unroll=UNROLL)
        def _(q):
            d = 2 * q + g + 1
            for hf in range(2):
                lo = hf * 64 + 8
                mid = slice(lo, lo + 64)
                c = psum[tile, d, xq, mid]
                before = psum[tile - 1, d, xq, mid] if tile > 0 else 0.0
                after = psum[tile + 1, d, xq, mid] if tile < NT - 1 else 0.0
                n = psum[tile, d, xq, slice(lo - 1, lo + 63)] + psum[tile, d, xq, slice(lo + 1, lo + 65)]
                n = n + (psum[tile, d - 1, xq, mid] + psum[tile, d + 1, xq, mid])
                n = n + (pltpu.roll(jnp.where(lane == CW - 1, before, c), 1, 1) +
                         pltpu.roll(jnp.where(lane == 0, after, c), CW - 1, 1))
                r = (6.0 * c - n).reshape(8, 8, CW)
                if tile == ZTILE:
                    for j in range(8):
                        LC[g, hf * 2 + j // 4, lax.rem(q, 2), (q // 2) * 8 + xq * 4 + j % 4] = r[j]
                elif g == 0:
                    L[0, ch, xq * 2 + q // 2, lax.rem(q, 2), pl.ds(hf * 8, 8)] = r
                else:
                    for j in range(8):
                        L[1, ch, j % 4, lax.rem(q, 2), (q // 2) * 8 + xq * 4 + hf * 2 + j // 4] = r[j]

    def relay(g, ch):
        for d, step in DIRS:
            send(L.at[g, ch, pos(g, 2), d], rel.at[g, ch, d], snd.at[1], rel_r.at[g, ch], peer(g, step))

    def direct(g, ch):
        for d, step in DIRS:
            send(L.at[g, ch, pos(g, step), 1 - d], inn.at[g, ch, 0, d], snd.at[2], in_r.at[g, ch], peer(g, step))

    def combine(g, ch):
        wait_in(rel.at[g, ch], rel_r.at[g, ch])
        for d, step in DIRS:
            rel[g, ch, d] = rel[g, ch, d] + L[g, ch, pos(g, step), d]
            send(rel.at[g, ch, d], inn.at[g, ch, 1, d], snd.at[2], in_r.at[g, ch], peer(g, step))

    def first_sum(g, ch):
        wait_in(inn.at[g, ch], in_r.at[g, ch])
        for h in range(2):
            total = (L[g, ch, pos(g, 0), h] + inn[g, ch, 0, 1 - h]) + inn[g, ch, 1, h]
            for j in range(16):
                if g == 0:
                    S[g, ch, j % 4, h, j // 4] = total[j]
                else:
                    S[g, ch, (j // 4 % 2) * 2 + j // 8, h, j % 4] = total[j]

    def second_send(g, ch):
        o = 1 - g
        if ch == NCH - 1:
            for j, step in enumerate((2, 1, -1)):
                send(S.at[g, ch, pos(o, step)], qall.at[g, j], snd.at[5], qall_r.at[g], peer(o, step))
            return
        for d, step in DIRS:
            send(S.at[g, ch, pos(o, 2), d], qrel.at[g, ch, d], snd.at[3], qrel_r.at[g, ch], peer(o, step))
        for d, step in DIRS:
            send(S.at[g, ch, pos(o, step), 1 - d], qinn.at[g, ch, 0, d], snd.at[4], qin_r.at[g, ch], peer(o, step))

    def second_combine(g, ch):
        o = 1 - g
        wait_in(qrel.at[g, ch], qrel_r.at[g, ch])
        for d, step in DIRS:
            qrel[g, ch, d] = qrel[g, ch, d] + S[g, ch, pos(o, step), d]
            send(qrel.at[g, ch, d], qinn.at[g, ch, 1, d], snd.at[4], qin_r.at[g, ch], peer(o, step))

    def second_sum(g, ch):
        own = S[g, ch, pos(1 - g, 0)]
        if ch == NCH - 1:
            wait_in(qall.at[g], qall_r.at[g])
            total = (own + qall[g, 0]) + (qall[g, 1] + qall[g, 2])
            for h in range(2):
                for j in range(4):
                    T[ch, h, j, g] = total[h, j]
            return
        wait_in(qinn.at[g, ch], qin_r.at[g, ch])
        for h in range(2):
            total = (own[h] + qinn[g, ch, 0, 1 - h]) + qinn[g, ch, 1, h]
            for j in range(4):
                T[ch, h, j, g] = total[j]

    def third_send(ch):
        for k in (2, 1, 3, 0):
            j = lax.rem(z + k, 4)
            zq = core * 4 + j
            for cq in range(2):
                send_if(jnp.logical_or(zq != z, core != cq), T.at[ch, cq, j], zin.at[ch, z], snd.at[6], z_r.at[ch],
                        at(X, zq, y, cq))

        @pl.when(holds)
        def _():
            zin[ch, z] = T[ch, core, lax.rem(z, 4)]

    def third_sum(ch):
        @pl.when(holds)
        def _():
            wait_in(zin.at[ch, pl.ds(0, 7)], z_r.at[ch])

        @pl.when(jnp.logical_not(holds))
        def _():
            wait_in(zin.at[ch], z_r.at[ch])

        total = (zin[ch, 0] + zin[ch, 1]) + (zin[ch, 2] + zin[ch, 3])
        total = total + ((zin[ch, 4] + zin[ch, 5]) + (zin[ch, 6] + zin[ch, 7]))
        out[:, :, TILES[ch] * CW:(TILES[ch] + 1) * CW] = total * scale

    def z_active(j, step):
        dest = wrap(z + step * (5 - j), 8)
        return dest // 4 == core, lax.rem(dest, 4)

    def z_stage(j):
        for g in range(2):
            for d, step in DIRS:
                active, block = z_active(j, step)
                if j == 1:
                    send_if(active, LC.at[g, block, d], zc.at[d, 0, g, d], zc_s.at[d, 0], zc_r.at[d, 0, g], zring[d])
                    continue

                @pl.when(active)
                def _():
                    if j == 2:
                        wait_in(zc.at[d, 0, g, d], zc_r.at[d, 0, g])
                        LC[g, block, d] = LC[g, block, d] + zc[d, 0, g, d]
                    else:
                        wait_in(zc.at[d, j - 2, g], zc_r.at[d, j - 2, g])
                        LC[g, block] = LC[g, block] + zc[d, j - 2, g]
                    send(LC.at[g, block], zc.at[d, j - 1, g], zc_s.at[d, j - 1], zc_r.at[d, j - 1, g], zring[d])

    def z_final():
        block = lax.rem(z, 4)

        @pl.when(holds)
        def _():
            for g in range(2):
                for d in range(2):
                    wait_in(zc.at[d, 3, g], zc_r.at[d, 3, g])

                @pl.loop(0, 16)
                def _(i):
                    for cq in range(2):
                        R[cq * 16 + i, g] = (LC[g, block, cq, i] + zc[0, 3, g, cq, i]) + zc[1, 3, g, cq, i]

            xyin[me] = R[core * 16 + lax.rem(X, 2) * 8 + (X // 2) * 4 + y]
            for a in (2, 1, 3, 0):
                for b in (2, 1, 3, 0):
                    Xq, yq = wrap(X + a, 4), wrap(y + b, 4)
                    i = lax.rem(Xq, 2) * 8 + (Xq // 2) * 4 + yq
                    for cq in range(2):
                        if a or b:
                            send(R.at[cq * 16 + i], xyin.at[me], snd.at[7], xy_r, at(Xq, z, yq, cq))
                        else:
                            send_if(core != cq, R.at[cq * 16 + i], xyin.at[me], snd.at[7], xy_r, at(Xq, z, yq, cq))

    def xy_sum():
        @pl.when(holds)
        def _():
            wait_in(xyin.at[pl.ds(0, 15)], xy_r)

        @pl.when(jnp.logical_not(holds))
        def _():
            wait_in(xyin, xy_r)

        parts = [xyin[k] for k in range(16)]
        while len(parts) > 1:
            parts = [parts[k] + parts[k + 1] for k in range(0, len(parts), 2)]
        out[:, :, ZTILE * CW:(ZTILE + 1) * CW] = parts[0] * scale

    def each(fn, ch):
        for g in range(2):
            fn(g, ch)

    def begin(ch):
        for g in range(2):
            for xq in range(2):
                stencil(TILES[ch], g, xq)
            relay(g, ch)

    pair(0)
    stencil(0, 0, far)
    relay(0, 0)
    pair(2)
    hand_over(4)
    stencil(0, 1, far)
    stencil(0, 1, near)
    relay(1, 0)
    direct(1, 0)
    stencil(0, 0, near)
    direct(0, 0)
    hand_over(6)
    pair(4)
    for g in range(2):
        for xq in range(2):
            stencil(ZTILE, g, xq)
    z_stage(1)
    pair(6)
    begin(1)
    each(combine, 0)
    each(direct, 1)
    pass_token(0)
    z_stage(2)
    begin(2)
    each(combine, 1)
    each(direct, 2)
    pass_token(1)
    each(first_sum, 0)
    each(second_send, 0)
    z_stage(3)
    each(combine, 2)
    pass_token(2)
    each(first_sum, 1)
    each(second_send, 1)
    each(second_combine, 0)
    z_stage(4)
    each(first_sum, 2)
    each(second_send, 2)
    each(second_combine, 1)
    each(second_sum, 0)
    pass_token(3)
    third_send(0)
    z_final()
    each(second_sum, 1)
    third_send(1)
    each(second_sum, 2)
    third_send(2)
    third_sum(0)
    third_sum(1)
    xy_sum()
    third_sum(2)
    for k, buffer in enumerate((theirs, rel, inn, qrel, qinn, qall)):
        wait_in(buffer, snd.at[k])

    @pl.when(holds)
    def _():
        wait_in(zin.at[:, pl.ds(0, 7)], snd.at[6])
        wait_in(R.at[pl.ds(0, 31)], snd.at[7])

    @pl.when(jnp.logical_not(holds))
    def _():
        wait_in(zin, snd.at[6])

    for j in range(1, 5):
        for d, step in DIRS:
            @pl.when(z_active(j, step)[0])
            def _():
                sent = zc.at[d, 0, 0] if j == 1 else zc.at[d, j - 1]
                wait_in(sent, zc_s.at[d, j - 1])


def solution(mesh):
    shots = mesh.shape["shot"] * mesh.shape["tile"]
    scale = 1.0 / float(shots) ** 0.5
    D = pltpu.SemaphoreType.DMA
    V = pltpu.VMEM

    def step(partials):
        return pl.pallas_call(
            functools.partial(kernel, scale),
            out_shape=jax.ShapeDtypeStruct((2, 8, NY), F32),
            in_specs=[pl.BlockSpec(memory_space=pl.ANY)],
            out_specs=pl.BlockSpec(memory_space=pltpu.VMEM),
            scratch_shapes=[
                V((NT, 2, 8, 18, 8, CW), BF16),
                V((NT, 2, 8, 18, 8, CW), BF16),
                V((NT, 2, 8, 18, 8, CW), BF16),
                V((NT, 10, 2, 144, CW), F32),
                V((2, NCH, 4, 2, 16, 8, CW), F32),
                V((2, NCH, 2, 16, 8, CW), F32),
                V((2, NCH, 2, 2, 16, 8, CW), F32),
                V((2, NCH, 4, 2, 4, 8, CW), F32),
                V((2, NCH - 1, 2, 4, 8, CW), F32),
                V((2, NCH - 1, 2, 2, 4, 8, CW), F32),
                V((2, 3, 2, 4, 8, CW), F32),
                V((NCH, 2, 4, 2, 8, CW), F32),
                V((NCH, 8, 2, 8, CW), F32),
                V((2, 4, 2, 16, 8, CW), F32),
                V((2, 4, 2, 2, 16, 8, CW), F32),
                V((32, 2, 8, CW), F32),
                V((16, 2, 8, CW), F32),
                D((NT, 2)), D((NT, 2)), D((NT, 2)),
                D((2, NCH)), D((2, NCH)),
                D((2, NCH - 1)), D((2, NCH - 1)), D((2,)),
                D((NCH,)), D((2, 4, 2)), D(()),
                D((8,)), D((2, 4)),
                pltpu.SemaphoreType.REGULAR((4,)),
            ],
            compiler_params=pltpu.CompilerParams(collective_id=0, has_side_effects=True,
                                                 vmem_limit_bytes=52 * 1024 * 1024),
        )(partials.reshape(8, 64, 8, NY))

    return jax.shard_map(step, mesh=mesh, in_specs=(P(("shot", "tile"), None, None, None),),
                         out_specs=P("shot", "tile", None), check_vma=False)
```

time: 43.4 us -> 41.3 us (0.952)
  Pallas kernels: 42.7 us -> 40.6 us
    pallas_call x1, Pallas kernels: 42.7 us -> 40.6 us  [step(): pl.pallas_call(functools.partial(kernel, scale), out_shape=jax.ShapeDtype...]
where the time goes in v6:
time: 41.3 us; the launch traced here: 41.2 us
  Pallas kernels  40.6 us (98%)
  local copies, waits for them, and re-layouts  0.62 us (2%)
    pallas_call x1, Pallas kernels, step(): pl.pallas_call(functools.partial(kernel, scale), out_shape=jax.ShapeDtype...  40.6 us

profile of v6, /device:TPU:1, one launch (start us, length us, event | category | flops | bytes accessed | tf_op | source)
XLA Modules:
  0.0 41.2 jit_solution(17609850745597905363)
XLA Ops:
  0.0 40.6 %shard_map.17 = f32[2,8,512]{2,1,0:T(8,128)S(1)} custom-call(bf16[8,64,8,512]{3,2,1,0:T(8,128)(2,1)} %bitcast.1), custom_call_target="tpu_custom_call" | custom-call | tf_op jit(solution)/shard_map/pallas_call | solution.py:385
  40.6 0.6 %copy.3 = f32[2,8,512]{2,1,0:T(8,128)} copy(f32[2,8,512]{2,1,0:T(8,128)S(1)} %shard_map.17) | data formatting | bytes 65536

commit v7 on v6

--- a/solution.py
+++ b/solution.py
@@ -11,10 +11,10 @@
 NY = 512
 CW = 128
 NT = NY // CW
-TILES = (0, 2, 3)
-ZTILE = 1
+TILES = (0, 1, 3)
+ZTILE = 2
 NCH = len(TILES)
-UNROLL = 2
+UNROLL = 4
 F32 = jnp.float32
 BF16 = jnp.bfloat16
 
@@ -104,8 +104,8 @@
             send(give.at[tile, xq], theirs.at[tile, xq], snd.at[0], th_r.at[tile, xq], sibling)
 
     hand_over(0)
+    load_both(4)
     hand_over(2)
-    load_both(4)
     load_both(6)
     token(0, zring)
 
@@ -118,7 +118,7 @@
             low = jnp.where(jnp.logical_and(core == 0, xq == 0), 0.0, 1.0).astype(F32)
             high = jnp.where(jnp.logical_and(core == 1, xq == 1), 0.0, 1.0).astype(F32)
 
-            @pl.loop(0, 8)
+            @pl.loop(0, 8, unroll=4)
             def _(d):
                 v = (mine[tile, xq, d].astype(F32) + theirs[tile, xq, d].astype(F32)).reshape(144, CW)
                 psum[tile, d + 1, xq, 8:136] = v[8:136]
@@ -237,23 +237,18 @@
         dest = wrap(z + step * (5 - j), 8)
         return dest // 4 == core, lax.rem(dest, 4)
 
-    def z_stage(j):
+    def z_part(j, short):
         for g in range(2):
             for d, step in DIRS:
                 active, block = z_active(j, step)
-                if j == 1:
-                    send_if(active, LC.at[g, block, d], zc.at[d, 0, g, d], zc_s.at[d, 0], zc_r.at[d, 0, g], zring[d])
-                    continue
+                cq = 1 - d if short else d
 
                 @pl.when(active)
                 def _():
-                    if j == 2:
-                        wait_in(zc.at[d, 0, g, d], zc_r.at[d, 0, g])
-                        LC[g, block, d] = LC[g, block, d] + zc[d, 0, g, d]
-                    else:
-                        wait_in(zc.at[d, j - 2, g], zc_r.at[d, j - 2, g])
-                        LC[g, block] = LC[g, block] + zc[d, j - 2, g]
-                    send(LC.at[g, block], zc.at[d, j - 1, g], zc_s.at[d, j - 1], zc_r.at[d, j - 1, g], zring[d])
+                    if j > 1 + short:
+                        wait_in(zc.at[d, j - 2, g, cq], zc_r.at[d, j - 2, g, cq])
+                        LC[g, block, cq] = LC[g, block, cq] + zc[d, j - 2, g, cq]
+                    send(LC.at[g, block, cq], zc.at[d, j - 1, g, cq], zc_s.at[d, j - 1], zc_r.at[d, j - 1, g, cq], zring[d])
 
     def z_final():
         block = lax.rem(z, 4)
@@ -262,7 +257,8 @@
         def _():
             for g in range(2):
                 for d in range(2):
-                    wait_in(zc.at[d, 3, g], zc_r.at[d, 3, g])
+                    for cq in range(2):
+                        wait_in(zc.at[d, 3, g, cq], zc_r.at[d, 3, g, cq])
 
                 @pl.loop(0, 16)
                 def _(i):
@@ -307,9 +303,9 @@
     pair(0)
     stencil(0, 0, far)
     relay(0, 0)
-    pair(2)
     hand_over(4)
     stencil(0, 1, far)
+    pair(2)
     stencil(0, 1, near)
     relay(1, 0)
     direct(1, 0)
@@ -317,32 +313,38 @@
     direct(0, 0)
     hand_over(6)
     pair(4)
-    for g in range(2):
-        for xq in range(2):
-            stencil(ZTILE, g, xq)
-    z_stage(1)
+    begin(1)
+    combine(0, 0)
+    direct(0, 1)
     pair(6)
-    begin(1)
-    each(combine, 0)
-    each(direct, 1)
+    stencil(ZTILE, 0, 0)
+    stencil(ZTILE, 0, 1)
+    combine(1, 0)
+    direct(1, 1)
+    stencil(ZTILE, 1, 0)
+    stencil(ZTILE, 1, 1)
+    z_part(1, 0)
     pass_token(0)
-    z_stage(2)
     begin(2)
+    z_part(2, 1)
     each(combine, 1)
     each(direct, 2)
+    z_part(2, 0)
     pass_token(1)
     each(first_sum, 0)
     each(second_send, 0)
-    z_stage(3)
+    z_part(3, 1)
     each(combine, 2)
+    z_part(3, 0)
     pass_token(2)
     each(first_sum, 1)
     each(second_send, 1)
+    z_part(4, 1)
     each(second_combine, 0)
-    z_stage(4)
+    z_part(4, 0)
+    each(second_combine, 1)
     each(first_sum, 2)
     each(second_send, 2)
-    each(second_combine, 1)
     each(second_sum, 0)
     pass_token(3)
     third_send(0)
@@ -408,7 +410,7 @@
                 D((NT, 2)), D((NT, 2)), D((NT, 2)),
                 D((2, NCH)), D((2, NCH)),
                 D((2, NCH - 1)), D((2, NCH - 1)), D((2,)),
-                D((NCH,)), D((2, 4, 2)), D(()),
+                D((NCH,)), D((2, 4, 2, 2)), D(()),
                 D((8,)), D((2, 4)),
                 pltpu.SemaphoreType.REGULAR((4,)),
             ],

time: 41.3 us -> 40.3 us (0.976)
  Pallas kernels: 40.6 us -> 39.6 us
    pallas_call x1, Pallas kernels: 40.6 us -> 39.6 us  [step(): pl.pallas_call(functools.partial(kernel, scale), out_shape=jax.ShapeDtype...]
where the time goes in v7:
time: 40.3 us; the launch traced here: 40.2 us
  Pallas kernels  39.6 us (98%)
  local copies, waits for them, and re-layouts  0.62 us (2%)
    pallas_call x1, Pallas kernels, step(): pl.pallas_call(functools.partial(kernel, scale), out_shape=jax.ShapeDtype...  39.6 us

profile of v7, /device:TPU:1, one launch (start us, length us, event | category | flops | bytes accessed | tf_op | source)
XLA Modules:
  0.0 40.2 jit_solution(8342665139467546287)
XLA Ops:
  0.0 39.6 %shard_map.17 = f32[2,8,512]{2,1,0:T(8,128)S(1)} custom-call(bf16[8,64,8,512]{3,2,1,0:T(8,128)(2,1)} %bitcast.1), custom_call_target="tpu_custom_call" | custom-call | tf_op jit(solution)/shard_map/pallas_call | solution.py:387
  39.6 0.6 %copy.3 = f32[2,8,512]{2,1,0:T(8,128)} copy(f32[2,8,512]{2,1,0:T(8,128)S(1)} %shard_map.17) | data formatting | bytes 65536

commit v8 on v7

--- a/solution.py
+++ b/solution.py
@@ -11,8 +11,8 @@
 NY = 512
 CW = 128
 NT = NY // CW
-TILES = (0, 1, 3)
-ZTILE = 2
+TILES = (0, 2, 3)
+ZTILE = 1
 NCH = len(TILES)
 UNROLL = 4
 F32 = jnp.float32
@@ -68,10 +68,6 @@
 
     load_both(0)
     load_both(2)
-    for tile in range(NT):
-        for xq in range(2):
-            psum[tile, 0, xq] = jnp.zeros((144, CW), F32)
-            psum[tile, 9, xq] = jnp.zeros((144, CW), F32)
     pl.semaphore_wait(barrier, 7)
 
     def token(k, devices):
@@ -108,6 +104,10 @@
     hand_over(2)
     load_both(6)
     token(0, zring)
+    for tile in range(NT):
+        for xq in range(2):
+            psum[tile, 0, xq] = jnp.zeros((144, CW), F32)
+            psum[tile, 9, xq] = jnp.zeros((144, CW), F32)
 
     lane = lax.broadcasted_iota(jnp.int32, (64, CW), 1)
 
@@ -177,9 +177,9 @@
 
     def second_send(g, ch):
         o = 1 - g
-        if ch == NCH - 1:
+        if ch > 0:
             for j, step in enumerate((2, 1, -1)):
-                send(S.at[g, ch, pos(o, step)], qall.at[g, j], snd.at[5], qall_r.at[g], peer(o, step))
+                send(S.at[g, ch, pos(o, step)], qall.at[g, ch - 1, j], snd.at[5], qall_r.at[g, ch - 1], peer(o, step))
             return
         for d, step in DIRS:
             send(S.at[g, ch, pos(o, 2), d], qrel.at[g, ch, d], snd.at[3], qrel_r.at[g, ch], peer(o, step))
@@ -195,9 +195,9 @@
 
     def second_sum(g, ch):
         own = S[g, ch, pos(1 - g, 0)]
-        if ch == NCH - 1:
-            wait_in(qall.at[g], qall_r.at[g])
-            total = (own + qall[g, 0]) + (qall[g, 1] + qall[g, 2])
+        if ch > 0:
+            wait_in(qall.at[g, ch - 1], qall_r.at[g, ch - 1])
+            total = (own + qall[g, ch - 1, 0]) + (qall[g, ch - 1, 1] + qall[g, ch - 1, 2])
             for h in range(2):
                 for j in range(4):
                     T[ch, h, j, g] = total[h, j]
@@ -209,7 +209,7 @@
                 T[ch, h, j, g] = total[j]
 
     def third_send(ch):
-        for k in (2, 1, 3, 0):
+        for k in (0, 2, 1, 3):
             j = lax.rem(z + k, 4)
             zq = core * 4 + j
             for cq in range(2):
@@ -313,36 +313,35 @@
     direct(0, 0)
     hand_over(6)
     pair(4)
-    begin(1)
-    combine(0, 0)
-    direct(0, 1)
-    pair(6)
     stencil(ZTILE, 0, 0)
     stencil(ZTILE, 0, 1)
-    combine(1, 0)
-    direct(1, 1)
     stencil(ZTILE, 1, 0)
     stencil(ZTILE, 1, 1)
     z_part(1, 0)
+    pair(6)
+    begin(1)
+    z_part(2, 1)
+    combine(0, 0)
+    direct(0, 1)
+    combine(1, 0)
+    direct(1, 1)
     pass_token(0)
     begin(2)
-    z_part(2, 1)
+    z_part(2, 0)
     each(combine, 1)
     each(direct, 2)
-    z_part(2, 0)
     pass_token(1)
+    z_part(3, 1)
     each(first_sum, 0)
     each(second_send, 0)
-    z_part(3, 1)
+    z_part(3, 0)
     each(combine, 2)
-    z_part(3, 0)
     pass_token(2)
+    z_part(4, 1)
     each(first_sum, 1)
     each(second_send, 1)
-    z_part(4, 1)
+    z_part(4, 0)
     each(second_combine, 0)
-    z_part(4, 0)
-    each(second_combine, 1)
     each(first_sum, 2)
     each(second_send, 2)
     each(second_sum, 0)
@@ -398,9 +397,9 @@
                 V((2, NCH, 2, 16, 8, CW), F32),
                 V((2, NCH, 2, 2, 16, 8, CW), F32),
                 V((2, NCH, 4, 2, 4, 8, CW), F32),
-                V((2, NCH - 1, 2, 4, 8, CW), F32),
-                V((2, NCH - 1, 2, 2, 4, 8, CW), F32),
-                V((2, 3, 2, 4, 8, CW), F32),
+                V((2, 1, 2, 4, 8, CW), F32),
+                V((2, 1, 2, 2, 4, 8, CW), F32),
+                V((2, 2, 3, 2, 4, 8, CW), F32),
                 V((NCH, 2, 4, 2, 8, CW), F32),
                 V((NCH, 8, 2, 8, CW), F32),
                 V((2, 4, 2, 16, 8, CW), F32),
@@ -409,7 +408,7 @@
                 V((16, 2, 8, CW), F32),
                 D((NT, 2)), D((NT, 2)), D((NT, 2)),
                 D((2, NCH)), D((2, NCH)),
-                D((2, NCH - 1)), D((2, NCH - 1)), D((2,)),
+                D((2, 1)), D((2, 1)), D((2, 2)),
                 D((NCH,)), D((2, 4, 2, 2)), D(()),
                 D((8,)), D((2, 4)),
                 pltpu.SemaphoreType.REGULAR((4,)),

time: 40.3 us -> 39.4 us (0.978)
  Pallas kernels: 39.6 us -> 38.7 us
    pallas_call x1, Pallas kernels: 39.6 us -> 38.7 us  [step(): pl.pallas_call(functools.partial(kernel, scale), out_shape=jax.ShapeDtype...]
where the time goes in v8:
time: 39.4 us; the launch traced here: 39.3 us
  Pallas kernels  38.7 us (98%)
  local copies, waits for them, and re-layouts  0.62 us (2%)
    pallas_call x1, Pallas kernels, step(): pl.pallas_call(functools.partial(kernel, scale), out_shape=jax.ShapeDtype...  38.7 us

profile of v8, /device:TPU:1, one launch (start us, length us, event | category | flops | bytes accessed | tf_op | source)
XLA Modules:
  0.0 39.3 jit_solution(4344046002105350697)
XLA Ops:
  0.0 38.7 %shard_map.17 = f32[2,8,512]{2,1,0:T(8,128)S(1)} custom-call(bf16[8,64,8,512]{3,2,1,0:T(8,128)(2,1)} %bitcast.1), custom_call_target="tpu_custom_call" | custom-call | tf_op jit(solution)/shard_map/pallas_call | solution.py:386
  38.7 0.6 %copy.3 = f32[2,8,512]{2,1,0:T(8,128)} copy(f32[2,8,512]{2,1,0:T(8,128)S(1)} %shard_map.17) | data formatting | bytes 65536

commit v9 on v8

--- a/solution.py
+++ b/solution.py
@@ -177,6 +177,12 @@
 
     def second_send(g, ch):
         o = 1 - g
+        if ch == NCH - 1:
+            for h in range(2):
+                for j, step in enumerate((2, 1, -1)):
+                    send(S.at[g, ch, pos(o, step), h], qall.at[g, ch - 1, j, h], snd.at[5], qall_r.at[g, ch - 1 + h],
+                         peer(o, step))
+            return
         if ch > 0:
             for j, step in enumerate((2, 1, -1)):
                 send(S.at[g, ch, pos(o, step)], qall.at[g, ch - 1, j], snd.at[5], qall_r.at[g, ch - 1], peer(o, step))
@@ -208,17 +214,26 @@
             for j in range(4):
                 T[ch, h, j, g] = total[j]
 
-    def third_send(ch):
+    def last_sum(h):
+        k = NCH - 2
+        for g in range(2):
+            wait_in(qall.at[g, k, :, h], qall_r.at[g, k + h])
+            total = (S[g, NCH - 1, pos(1 - g, 0), h] + qall[g, k, 0, h]) + (qall[g, k, 1, h] + qall[g, k, 2, h])
+            for j in range(4):
+                T[NCH - 1, h, j, g] = total[j]
+
+    def third_send(ch, cores=(0, 1)):
         for k in (0, 2, 1, 3):
             j = lax.rem(z + k, 4)
             zq = core * 4 + j
-            for cq in range(2):
+            for cq in cores:
                 send_if(jnp.logical_or(zq != z, core != cq), T.at[ch, cq, j], zin.at[ch, z], snd.at[6], z_r.at[ch],
                         at(X, zq, y, cq))
 
-        @pl.when(holds)
-        def _():
-            zin[ch, z] = T[ch, core, lax.rem(z, 4)]
+        if 1 in cores:
+            @pl.when(holds)
+            def _():
+                zin[ch, z] = T[ch, core, lax.rem(z, 4)]
 
     def third_sum(ch):
         @pl.when(holds)
@@ -350,8 +365,9 @@
     z_final()
     each(second_sum, 1)
     third_send(1)
-    each(second_sum, 2)
-    third_send(2)
+    for h in range(2):
+        last_sum(h)
+        third_send(2, (h,))
     third_sum(0)
     third_sum(1)
     xy_sum()
@@ -408,7 +424,7 @@
                 V((16, 2, 8, CW), F32),
                 D((NT, 2)), D((NT, 2)), D((NT, 2)),
                 D((2, NCH)), D((2, NCH)),
-                D((2, 1)), D((2, 1)), D((2, 2)),
+                D((2, 1)), D((2, 1)), D((2, 3)),
                 D((NCH,)), D((2, 4, 2, 2)), D(()),
                 D((8,)), D((2, 4)),
                 pltpu.SemaphoreType.REGULAR((4,)),

time: 39.4 us -> 39 us (0.990)
  Pallas kernels: 38.7 us -> 38.3 us
where the time goes in v9:
time: 39 us
  Pallas kernels  38.3 us (98%)
  local copies, waits for them, and re-layouts  0.62 us (2%)
    pallas_call x1, Pallas kernels, step(): pl.pallas_call(functools.partial(kernel, scale), out_shape=jax.ShapeDtype...  38.3 us

profile of v9, /device:TPU:1, one launch (start us, length us, event | category | flops | bytes accessed | tf_op | source)
XLA Modules:
  0.0 39.0 jit_solution(13630337547908889139)
XLA Ops:
  0.0 38.3 %shard_map.17 = f32[2,8,512]{2,1,0:T(8,128)S(1)} custom-call(bf16[8,64,8,512]{3,2,1,0:T(8,128)(2,1)} %bitcast.1), custom_call_target="tpu_custom_call" | custom-call | tf_op jit(solution)/shard_map/pallas_call | solution.py:402
  38.3 0.6 %copy.3 = f32[2,8,512]{2,1,0:T(8,128)} copy(f32[2,8,512]{2,1,0:T(8,128)S(1)} %shard_map.17) | data formatting | bytes 65536
